TPU v7x, 256 devices: a whole 4x4x8 slice. The times are simulated.
256 devices in a mesh: dp: 32 (over z, y), mp: 8 (over x, core).
Axes of the slice: x: 4, y: 4, z: 8, core: 2. Of those that a mesh axis runs over, the one named last changes fastest.
Arguments:
- residual_input: bfloat16 [8192, 5120], P('dp', 'mp'), may hold values from -6 to 6
- cotangent: bfloat16 [8192, 5120], P('dp', 'mp'), may hold values from -0.6 to 0.6
- lengths: int32 [32], P('dp'), may hold values from 64 to 256
- norm_gain_vector: bfloat16 [5120], replicated, may hold values from 0.5 to 1.5
- gate_projection_weight: bfloat16 [5120, 6912], P('dp', 'mp'), may hold values from -0.078125 to 0.078125
- up_projection_weight: bfloat16 [5120, 6912], P('dp', 'mp'), may hold values from -0.078125 to 0.078125
- down_projection_weight: bfloat16 [5120, 6912], P('dp', 'mp'), may hold values from -0.078125 to 0.078125
- up_adapter_first: bfloat16 [5120, 16], replicated, may hold values from -0.078125 to 0.078125
- up_adapter_second: bfloat16 [16, 6912], P(None, 'mp'), may hold values from -0.29882812 to 0.29882812
- down_adapter_first: bfloat16 [6912, 16], P('mp'), may hold values from -0.078125 to 0.078125
- down_adapter_second: bfloat16 [16, 5120], replicated, may hold values from -0.29882812 to 0.29882812
Outputs:
- up_first_gradient: float32 [5120, 16], P('dp')
- up_second_gradient: float32 [16, 6912], P(None, ('mp', 'dp'))
- down_first_gradient: float32 [6912, 16], P(('mp', 'dp'))
- down_second_gradient: float32 [16, 5120], P(None, 'dp')
All inputs are finite; a program needn't handle non-finite values.
Results may differ from a plain program's by a relative error of at most 0.0061.
Values may be sent and summed in bfloat16 or wider, within the bound.
A program may use at most 128 MiB of HBM per device.

v0:
```python
import math

import jax
import jax.numpy as jnp
from jax import lax
from jax.sharding import PartitionSpec as P

MODEL_WIDTH = 5120
HIDDEN_SHARD = 6912
ADAPTER_RANK = 16


norm_eps = 1e-06
adapter_scale = 2.0
clip_coefficient = 0.005


def side_by_side(arrays, axis, dim, along):
    ends, at = ([], 0)
    for a in arrays[:-1]:
        at += a.shape[along]
        ends.append(at)
    both = jnp.concatenate(arrays, axis=along)
    return tuple(jnp.split(lax.all_gather(both, axis, axis=dim, tiled=True), ends, axis=along))


def in_blocks(x, dim, length):
    dims = x.shape
    parts = x.reshape(*dims[:dim], length, dims[dim] // length, *dims[dim + 1 :])
    return jnp.moveaxis(parts, dim, 0)


def sent_and_summed(x, axis, dim):
    parts = in_blocks(x, dim, lax.axis_size(axis))
    arrived = lax.all_to_all(parts, axis, split_axis=0, concat_axis=0, tiled=True)
    return arrived.sum(axis=0)


def fold_rows(left, piece):
    return jnp.dot(left, piece, preferred_element_type=jnp.float32)


def contract_row_dims(left, right):
    return lax.dot_general(
        left, right, (((0,), (0,)), ((), ())), preferred_element_type=jnp.float32
    )


def contract_columns(left, right):
    return lax.dot_general(
        left, right, (((1,), (1,)), ((), ())), preferred_element_type=jnp.float32
    )


def per_device(
    residual_input,
    cotangent,
    lengths,
    norm_gain_vector,
    gate_projection_weight,
    up_projection_weight,
    down_projection_weight,
    up_adapter_first,
    up_adapter_second,
    down_adapter_first,
    down_adapter_second,
):
    clip_limit = clip_coefficient * math.sqrt(2.0 * ADAPTER_RANK * (MODEL_WIDTH + HIDDEN_SHARD))
    rows, back_rows = side_by_side((residual_input, cotangent), "mp", 1, 0)
    seq = rows.shape[0]
    positions = lax.broadcasted_iota(jnp.int32, (seq, 1), 0)
    live = (positions < lengths[0]).astype(jnp.float32)
    output_gradient = (back_rows.astype(jnp.float32) * live).astype(jnp.bfloat16)
    wide = rows.astype(jnp.float32)
    inverse = lax.rsqrt(jnp.mean(wide * wide, axis=1, keepdims=True) + norm_eps)
    normalized_input = (wide * inverse * norm_gain_vector.astype(jnp.float32)).astype(jnp.bfloat16)
    up_adapter_latent = jnp.dot(
        normalized_input, up_adapter_first, preferred_element_type=jnp.float32
    ).astype(jnp.bfloat16)
    pieces = side_by_side(
        (gate_projection_weight, up_projection_weight, down_projection_weight), "dp", 0, 1
    )
    gate = fold_rows(normalized_input, pieces[0])
    up_frozen_output = fold_rows(normalized_input, pieces[1])
    backward_frozen = fold_rows(output_gradient, pieces[2])
    up_activation = up_frozen_output + adapter_scale * jnp.dot(
        up_adapter_latent, up_adapter_second, preferred_element_type=jnp.float32
    )
    gate_act = jax.nn.silu(gate)
    hidden_activation = (gate_act * up_activation).astype(jnp.bfloat16)
    down_adapter_latent = lax.psum(
        jnp.dot(hidden_activation, down_adapter_first, preferred_element_type=jnp.float32), "mp"
    ).astype(jnp.bfloat16)
    down_second_gradient = adapter_scale * contract_row_dims(down_adapter_latent, output_gradient)
    backward_adapter = contract_columns(output_gradient, down_adapter_second).astype(jnp.bfloat16)
    down_first_gradient = adapter_scale * contract_row_dims(hidden_activation, backward_adapter)
    hidden_gradient = backward_frozen + adapter_scale * contract_columns(
        backward_adapter, down_adapter_first
    )
    up_gradient = (hidden_gradient * gate_act).astype(jnp.bfloat16)
    up_second_gradient = adapter_scale * contract_row_dims(up_adapter_latent, up_gradient)
    up_partial_output = contract_columns(up_gradient, up_adapter_second)
    shared = jnp.sum(down_first_gradient * down_first_gradient) + jnp.sum(
        up_second_gradient * up_second_gradient
    )
    up_summed, shared_total = lax.psum((up_partial_output, shared), "mp")
    up_adapter_hidden = up_summed.astype(jnp.bfloat16)
    up_first_gradient = adapter_scale * contract_row_dims(normalized_input, up_adapter_hidden)
    owned = jnp.sum(up_first_gradient * up_first_gradient) + jnp.sum(
        down_second_gradient * down_second_gradient
    )
    factor = jnp.minimum(1.0, clip_limit / (jnp.sqrt(owned + shared_total) + 1e-06))
    first_sums = (
        sent_and_summed(factor * up_first_gradient, "dp", 0),
        sent_and_summed(factor * down_first_gradient, "dp", 0),
    )
    second_sums = (
        sent_and_summed(factor * up_second_gradient, "dp", 1),
        sent_and_summed(factor * down_second_gradient, "dp", 1),
    )
    return (first_sums[0], second_sums[0], first_sums[1], second_sums[1])


def solution(mesh):
    return jax.shard_map(
        per_device,
        mesh=mesh,
        in_specs=(
            P("dp", "mp"),
            P("dp", "mp"),
            P("dp"),
            P(),
            P("dp", "mp"),
            P("dp", "mp"),
            P("dp", "mp"),
            P(),
            P(None, "mp"),
            P("mp", None),
            P(),
        ),
        out_specs=(P("dp", None), P(None, ("mp", "dp")), P(("mp", "dp"), None), P(None, "dp")),
        check_vma=False,
    )
```

profile of v0, /device:TPU:6, one launch (start us, length us, event | category | flops | bytes accessed | tf_op | source)
XLA Modules:
  0.0 395.5 jit_solution(3806109247370449109)
XLA Ops:
  7.2 2.0 pad_maximum_fusion
  9.3 2.3 concatenate.7
  13.1 36.8 %all-gather.3.cloned.1.call-done = bf16[512,5120]{1,0:T(8,128)(2,1)} async-done(((bf16[512,640]{1,0:T(8,128)(2,1)}), bf16[512,5120]{1,0:T(8,128)(2,1)}) %all-gather.3.cloned.1.call-update) | async-done | bytes 5242896 | tf_op jit(solution)/shard_map/all_gather | solution.py:24
  49.9 2.5 fusion.6
  52.4 2.6 fusion.8
  56.6 195.1 %all-gather.5.cloned.1.call-done = bf16[5120,2592]{1,0:T(8,128)(2,1)} async-done(((bf16[160,2592]{1,0:T(8,128)(2,1)}), bf16[5120,2592]{1,0:T(8,128)(2,1)}) %all-gather.5.cloned.1.call-update) | async-done | bytes 26542096 | tf_op jit(solution)/shard_map/all_gather | solution.py:24
  251.7 7.3 %divide_multiply_fusion = f32[256,864]{0,1:T(8,128)S(1)} fusion(bf16[256,5120]{1,0:T(8,128)(2,1)S(1)} %fusion.8, bf16[5120,2592]{1,0:T(8,128)(2,1)} %all-gather.5.cloned.1.call-done), kind=kOutput, calls=%fused_computation.22 | convolution fusion | flops 2265808896 | bytes 12681216 | tf_op jit(solution)/shard_map/dot_general | solution.py:40
  259.1 11.6 %fusion = f32[256,864]{0,1:T(8,128)S(1)} fusion(bf16[256,5120]{1,0:T(8,128)(2,1)S(1)} %fusion.8, bf16[5120,2592]{1,0:T(8,128)(2,1)} %all-gather.5.cloned.1.call-done), kind=kOutput, calls=%fused_computation | convolution fusion | flops 2264924160 | bytes 12681216 | tf_op jit(solution)/shard_map/dot_general | solution.py:40
  272.0 12.2 %fusion.4 = f32[256,864]{0,1:T(8,128)S(1)} fusion(bf16[5120,2592]{1,0:T(8,128)(2,1)} %all-gather.5.cloned.1.call-done, bf16[512,5120]{1,0:T(8,128)(2,1)} %all-gather.3.cloned.1.call-done, f32[256]{0:T(256)S(1)} %compare_convert_fusion), kind=kOutput, calls=%fused_computation.4 | convolution fusion | flops 2268856320 | bytes 12682240 | tf_op jit(solution)/shard_map/dot_general | solution.py:40
  286.9 22.9 %all-reduce = (bf16[256,16]{0,1:T(8,128)(2,1)S(1)}, bf16[256,16]{0,1:T(8,128)(2,1)}, f32[]{:T(128)}) all-reduce(f32[256,16]{0,1:T(8,128)S(1)} %fusion.21, f32[256,16]{0,1:T(8,128)S(1)} %fusion.22, f32[]{:T(128)S(6)} %add.45), channel_id=1, replica_groups=mesh['dp'=32,'mp'=8] {'mp'}, use_global_device_ids=true, to_apply=%region_1.2 | all-reduce | flops 8193 | bytes 49160 | tf_op jit(solution)/shard_map/psum | solution.py:106
  309.8 1.1 multiply_reduce_fusion.1
  310.9 3.0 multiply_reduce_fusion
  316.4 1.0 reshape.40
  317.3 5.9 %all-to-all-start.1 = ((f32[32,1,432]{2,1,0:T(1,128)}), f32[32,1,432]{2,1,0:T(1,128)S(1)}, u32[]{:S(2)}, u32[]{:S(2)}) async-start(f32[32,1,432]{2,1,0:T(1,128)} %reshape.40), calls=%async_computation.1 | async-start | bytes 131072 | tf_op jit(solution)/shard_map/all_to_all | solution.py:35
  323.7 1.0 reshape.42
  324.7 8.4 %all-to-all-done.1 = f32[32,1,432]{2,1,0:T(1,128)S(1)} async-done(((f32[32,1,432]{2,1,0:T(1,128)}), f32[32,1,432]{2,1,0:T(1,128)S(1)}, u32[]{:S(2)}, u32[]{:S(2)}) %all-to-all-start.1) | async-done | bytes 55328 | tf_op jit(solution)/shard_map/all_to_all | solution.py:35
  333.1 3.9 all-to-all-start.2
  337.3 1.1 copy.15
  338.4 8.6 %all-to-all-done.2 = f32[32,1,432]{2,1,0:T(1,128)S(1)} async-done(((f32[32,1,432]{2,1,0:T(1,128)}), f32[32,1,432]{2,1,0:T(1,128)S(1)}, u32[]{:S(2)}, u32[]{:S(2)}) %all-to-all-start.2) | async-done | bytes 55328 | tf_op jit(solution)/shard_map/all_to_all | solution.py:35
  347.0 3.9 all-to-all-start
  351.2 1.1 copy.21
  352.3 15.1 %all-to-all-done = f32[32,160,16]{1,2,0:T(8,128)S(1)} async-done(((f32[32,160,16]{1,2,0:T(8,128)}), f32[32,160,16]{1,2,0:T(8,128)S(1)}, u32[]{:S(2)}, u32[]{:S(2)}) %all-to-all-start) | async-done | bytes 327712 | tf_op jit(solution)/shard_map/all_to_all | solution.py:35
  367.4 4.3 %all-to-all-start.3 = ((f32[32,16,160]{2,1,0:T(8,128)}), f32[32,16,160]{2,1,0:T(8,128)S(1)}, u32[]{:S(2)}, u32[]{:S(2)}) async-start(f32[32,16,160]{2,1,0:T(8,128)} %bitcast.32), calls=%async_computation.3 | async-start | bytes 1048576 | tf_op jit(solution)/shard_map/all_to_all | solution.py:35
  376.1 12.0 %all-to-all-done.3 = f32[32,16,160]{2,1,0:T(8,128)S(1)} async-done(((f32[32,16,160]{2,1,0:T(8,128)}), f32[32,16,160]{2,1,0:T(8,128)S(1)}, u32[]{:S(2)}, u32[]{:S(2)}) %all-to-all-start.3) | async-done | bytes 327712 | tf_op jit(solution)/shard_map/all_to_all | solution.py:35
  (49 shorter events, 11.8 us)
Async XLA Ops:
  7.2 47.8 %copy-start = (bf16[5120,16]{0,1:T(8,128)(2,1)S(1)}, bf16[5120,16]{0,1:T(8,128)(2,1)}, u32[]{:S(2)}) copy-start(bf16[5120,16]{0,1:T(8,128)(2,1)} %param.18) | copy-start | bytes 491524
  7.2 42.7 %all-gather.3.cloned.1.call-start = ((), (), s32[]{:S(2)}) async-start(), calls=%async_computation.4 | async-start | bytes 5898240 | tf_op jit(solution)/shard_map/all_gather | solution.py:24
  9.3 242.5 %all-gather.5.cloned.1.call-start = ((), (), s32[]{:S(2)}) async-start(), calls=%async_computation.5 | async-start | bytes 28385280 | tf_op jit(solution)/shard_map/all_gather | solution.py:24
  13.1 259.0 %copy-start.4 = (f32[256]{0:T(256)}, f32[256]{0:T(256)S(1)}, u32[]{:S(2)}) copy-start(f32[256]{0:T(256)S(1)} %compare_convert_fusion) | copy-start | bytes 3076
  13.1 42.7 %copy-start.3 = (bf16[16,5120]{1,0:T(8,128)(2,1)S(1)}, bf16[16,5120]{1,0:T(8,128)(2,1)}, u32[]{:S(2)}) copy-start(bf16[16,5120]{1,0:T(8,128)(2,1)} %param.21) | copy-start | bytes 491524
  49.9 5.9 %slice-start = ((s8[5242880]{0:T(1024)(128)(4,1)}), s8[4194304]{0:T(1024)(128)(4,1)S(1)}, s32[]{:S(2)}) async-start(s8[5242880]{0:T(1024)(128)(4,1)} %bitcast.35), calls=%async_computation.6 | async-start | bytes 8388608
  52.4 3.4 slice-start.1
  259.0 11.6 %copy-start.2 = (bf16[16,864]{1,0:T(8,128)(2,1)S(1)}, bf16[16,864]{1,0:T(8,128)(2,1)}, u32[]{:S(2)}) copy-start(bf16[16,864]{1,0:T(8,128)(2,1)} %param.19) | copy-start | bytes 82948
  259.0 11.9 %copy-start.1 = (bf16[864,16]{0,1:T(8,128)(2,1)S(1)}, bf16[864,16]{0,1:T(8,128)(2,1)}, u32[]{:S(2)}) copy-start(bf16[864,16]{0,1:T(8,128)(2,1)} %param.20) | copy-start | bytes 82948
  317.3 15.7 %all-to-all-start.1 = ((f32[32,1,432]{2,1,0:T(1,128)}), f32[32,1,432]{2,1,0:T(1,128)S(1)}, u32[]{:S(2)}, u32[]{:S(2)}) async-start(f32[32,1,432]{2,1,0:T(1,128)} %reshape.40), calls=%async_computation.1 | async-start | bytes 131072 | tf_op jit(solution)/shard_map/all_to_all | solution.py:35
  333.1 13.9 %all-to-all-start.2 = ((f32[32,1,432]{2,1,0:T(1,128)}), f32[32,1,432]{2,1,0:T(1,128)S(1)}, u32[]{:S(2)}, u32[]{:S(2)}) async-start(f32[32,1,432]{2,1,0:T(1,128)} %reshape.42), calls=%async_computation.2 | async-start | bytes 131072 | tf_op jit(solution)/shard_map/all_to_all | solution.py:35
  347.0 20.4 %all-to-all-start = ((f32[32,160,16]{1,2,0:T(8,128)}), f32[32,160,16]{1,2,0:T(8,128)S(1)}, u32[]{:S(2)}, u32[]{:S(2)}) async-start(f32[32,160,16]{1,2,0:T(8,128)} %copy.15), calls=%async_computation | async-start | bytes 1048576 | tf_op jit(solution)/shard_map/all_to_all | solution.py:35
  367.4 20.7 %all-to-all-start.3 = ((f32[32,16,160]{2,1,0:T(8,128)}), f32[32,16,160]{2,1,0:T(8,128)S(1)}, u32[]{:S(2)}, u32[]{:S(2)}) async-start(f32[32,16,160]{2,1,0:T(8,128)} %bitcast.32), calls=%async_computation.3 | async-start | bytes 1048576 | tf_op jit(solution)/shard_map/all_to_all | solution.py:35
Sparse Core Ops, SparseCore 0:
  9.8 39.9 all-gather.2
  52.4 199.2 all-gather.4
where the time goes:
time: 396 us
  waiting for transfers between devices  276 us (70%)
  matrix products  39.5 us (10%)
  blocking collectives  22.9 us (6%)
  between operations  18.3 us (5%)
  starting transfers between devices  18 us (5%)
  other arithmetic  12.1 us (3%)
  local copies, waits for them, and re-layouts  8.89 us (2%)
    all_gather x2, waiting for transfers between devices, side_by_side(): lax.all_gather(both, axis, axis=dim, tiled=True)  232 us
    all_to_all x4, waiting for transfers between devices, sent_and_summed(): lax.all_to_all(parts, axis, split_axis=0, concat_axis=0, tiled=True)  44 us
    dot_general x3, matrix products, fold_rows(): return jnp.dot(left, piece, preferred_element_type=jnp.float32)  31 us
    psum x1, blocking collectives, per_device(): up_summed, shared_total = lax.psum((up_partial_output, shared), 'mp')  22.9 us
    all_to_all x4, starting transfers between devices, sent_and_summed(): lax.all_to_all(parts, axis, split_axis=0, concat_axis=0, tiled=True)  17.9 us
  transfers between devices with their start and end apart: 6, of which 6 were waited for; matrix products, arithmetic and copies ran while one was open for 5% of the time, Pallas kernels for 0%

commit v1 on v0

v1 whole, which is shorter than its diff:
```python
import math

import jax
import jax.numpy as jnp
from jax import lax
from jax.experimental import pallas as pl
from jax.experimental.pallas import tpu as pltpu
from jax.sharding import PartitionSpec as P

MODEL_WIDTH = 5120
HIDDEN_SHARD = 6912
ADAPTER_RANK = 16

norm_eps = 1e-06
adapter_scale = 2.0
clip_coefficient = 0.005

NZ, NY, NX, NC = 8, 4, 4, 2
NMP = NX * NC
NDP = NZ * NY
ROWS = 160
KLEN = ROWS * NZ
SEQ = 256
COLS = 864
WIDE = 896
HALF = ROWS // 2

PIECES = ((0, 0, 0, 896), (1, 0, 0, 896), (2, 1, 0, 512), (2, 1, 512, 384))
RING = (((0, 0), (0, 1), (1, 0), (1, 1), (2, 0), (2, 1), (3, 0)), ((0, 0), (0, 1), (1, 0), (1, 1), (2, 0), (2, 1), (3, 1)))
MESH = pl.DeviceIdType.MESH
BF, F32 = jnp.bfloat16, jnp.float32


def contract_row_dims(left, right):
    return lax.dot_general(left, right, (((0,), (0,)), ((), ())), preferred_element_type=F32)


def contract_columns(left, right):
    return lax.dot_general(left, right, (((1,), (1,)), ((), ())), preferred_element_type=F32)


def remote(src, dst, send, recv, dp, mp):
    return pltpu.make_async_remote_copy(
        src_ref=src, dst_ref=dst, send_sem=send, recv_sem=recv, device_id={"dp": dp, "mp": mp}, device_id_type=MESH
    )


def signal(sem, dp, mp):
    pl.semaphore_signal(sem, inc=1, device_id={"dp": dp, "mp": mp}, device_id_type=MESH)


def products_kernel(
    at, wb, ps, c_out, p_out, a_all, b_all, cs2, cs1, cr2, cr1, p_all,
    bs, br, ays, ayr, loc, axs, axr, ads, adr, c2s, c2r, c1s, c1r, pss, psr,
):
    d, m = lax.axis_index("dp"), lax.axis_index("mp")
    z, y, x, c = d // NY, lax.rem(d, NY), m // NC, lax.rem(m, NC)

    def dp_of(zz, yy):
        return lax.rem(zz, NZ) * NY + lax.rem(yy, NY)

    def mp_of(xx, cc):
        return lax.rem(xx, NX) * NC + cc

    up_z, down_z = dp_of(z + 1, y), dp_of(z + NZ - 1, y)
    up_y, down_y = dp_of(z, y + 1), dp_of(z, y + NY - 1)
    up_x, down_x = mp_of(x + 1, c), mp_of(x + NX - 1, c)
    far_x = mp_of(x + 2, c)
    twin = mp_of(x, 1 - c)

    bar = pltpu.get_barrier_semaphore()
    signal(bar, up_z, m)
    signal(bar, down_z, m)
    for k in range(1, NY):
        signal(bar, dp_of(z, y + k), m)
    for k in range(1, NMP):
        signal(bar, d, lax.rem(m + k, NMP))
    pl.semaphore_wait(bar, 2 + NY - 1 + NMP - 1)

    def rows_of(zz, h, n):
        return pl.ds(pl.multiple_of(zz * ROWS + h * HALF, 16), n)

    def ring_copy(p, way, i):
        w, _, c0, n = PIECES[p]
        s, h = RING[way][i]
        src_z = lax.rem(z + (NZ - s if way == 0 else s), NZ)
        cols = pl.ds(c0, n)
        here = wb.at[w, pl.ds(h * HALF, HALF), cols] if s == 0 else b_all.at[w, rows_of(src_z, h, HALF), cols]
        there = b_all.at[w, rows_of(src_z, h, HALF), cols]
        return remote(here, there, bs.at[p, way, i], br.at[p, way, i], up_z if way == 0 else down_z, m)

    def ring_issue(p, i):
        for way in range(2):
            s, h = RING[way][i]
            if s:
                ring_copy(p, way, 2 * (s - 1) + h).wait_recv()
            ring_copy(p, way, i).start()

    def ring_finish(p):
        for way in range(2):
            for i in (5, 6) if way == 0 else (4, 6):
                ring_copy(p, way, i).wait_recv()

    def feats(mm):
        return pl.ds(pl.multiple_of(mm * ROWS, 16), ROWS)

    def y_copy(a, k):
        yy = lax.rem(y + k, NY)
        return remote(at.at[yy, a], a_all.at[y, a, feats(m), :], ays.at[a, k - 1], ayr.at[a, k - 1], dp_of(z, yy), m)

    def own_copy(a):
        return pltpu.make_async_copy(at.at[y, a], a_all.at[y, a, feats(m), :], loc.at[a])

    def block(a, mm, e0, ne):
        return a_all.at[pl.ds(e0, ne), a, feats(mm), :]

    def x_copy(a, i):
        mm, e0, ne, to = ((m, 0, 4, up_x), (m, 0, 4, down_x), (down_x, 0, 2, up_x), (up_x, 2, 2, down_x))[i]
        return remote(block(a, mm, e0, ne), block(a, mm, e0, ne), axs.at[a, i], axr.at[a, i], d, to)

    def core_copy(a, i):
        mm, e0, ne = ((m, 0, 4), (down_x, 0, 4), (up_x, 0, 4), (far_x, 0, 2), (far_x, 2, 2))[i]
        return remote(block(a, mm, e0, ne), block(a, mm, e0, ne), ads.at[a, i], adr.at[a, i], d, twin)

    def tokens_start(a):
        for k in (2, 1, 3):
            y_copy(a, k).start()
        own_copy(a).start()

    def tokens_x(a):
        own_copy(a).wait()
        for k in (1, 2, 3):
            y_copy(a, k).wait_recv()
        x_copy(a, 0).start()
        x_copy(a, 1).start()
        core_copy(a, 0).start()

    def tokens_on(a):
        x_copy(a, 0).wait_recv()
        x_copy(a, 2).start()
        x_copy(a, 1).wait_recv()
        x_copy(a, 3).start()
        core_copy(a, 1).start()
        core_copy(a, 2).start()

    def tokens_last(a):
        x_copy(a, 2).wait_recv()
        core_copy(a, 3).start()
        x_copy(a, 3).wait_recv()
        core_copy(a, 4).start()

    def tokens_done(a):
        for i in range(5):
            core_copy(a, i).wait_recv()

    def product(p, t, store):
        w, a, c0, n = PIECES[p]

        def tile(lo, size):
            acc = lax.dot_general(
                a_all[t, a], b_all[w, :, pl.ds(lo, size)], (((0,), (0,)), ((), ())), preferred_element_type=F32
            )
            store(w, lo, size, acc)

        def step(i, carry):
            tile(pl.multiple_of(c0 + i * 256, 128), 256)
            return carry

        lax.fori_loop(0, n // 256, step, 0)
        if n % 256:
            tile(c0 + n - n % 256, n % 256)

    def half_copy(p, way):
        w, _, c0, n = PIECES[p]
        cols = pl.ds(c0, n)
        return remote(
            cs2.at[w, way, :, cols], cr2.at[w, way, :, cols], c2s.at[p, way], c2r.at[p, way], up_y if way == 0 else down_y, m
        )

    def full_copy(p, way, h):
        w, _, c0, n = PIECES[p]
        part = (way, pl.ds(h * 128, 128), pl.ds(c0, n))
        return remote(
            cs1.at[(w, *part)], cr1.at[(w, *part)], c1s.at[p, way, h], c1r.at[p, way, h], up_y if way == 0 else down_y, m
        )

    def unit_far(p):
        def store(w, lo, size, acc):
            v = acc.astype(BF)
            cs2[w, 0, :, pl.ds(lo, size)] = v[:128]
            cs2[w, 1, :, pl.ds(lo, size)] = v[128:]

        product(p, lax.rem(y + 2, NY), store)
        half_copy(p, 0).start()
        half_copy(p, 1).start()

    def unit_near(p, way):
        def store(w, lo, size, acc):
            cs1[w, way, :, pl.ds(lo, size)] = acc.astype(BF)

        product(p, lax.rem(y + (1 if way == 0 else NY - 1), NY), store)
        full_copy(p, way, 1 - way).start()

    def unit_pass(p):
        w, _, c0, n = PIECES[p]
        for way in range(2):
            half_copy(p, way).wait_recv()
            at_rows, cols = pl.ds(way * 128, 128), pl.ds(c0, n)
            total = cs1[w, way, at_rows, cols].astype(F32) + cr2[w, way, :, cols].astype(F32)
            cs1[w, way, at_rows, cols] = total.astype(BF)
            full_copy(p, way, way).start()

    def unit_own(p):
        def store(w, lo, size, acc):
            c_out[w, :, pl.ds(lo, size)] = acc

        product(p, y, store)

    def unit_sum(p):
        w, _, c0, n = PIECES[p]
        cols = pl.ds(c0, n)
        for way in range(2):
            for h in range(2):
                full_copy(p, way, h).wait_recv()
        c_out[w, :, cols] += cr1[w, 0, :, cols].astype(F32) + cr1[w, 1, :, cols].astype(F32)

    def p_copy(k):
        return remote(ps, p_all.at[m], pss.at[k - 1], psr.at[k - 1], d, lax.rem(m + k, NMP))

    def own_rows():
        for w in range(3):
            b_all[w, rows_of(z, 0, ROWS), :] = wb[w]

    def units(p):
        return [
            lambda: unit_far(p),
            lambda: unit_near(p, 0),
            lambda: unit_near(p, 1),
            lambda: unit_pass(p),
            lambda: unit_own(p),
        ]

    plan = {(p, i): [] for p in range(4) for i in range(7)}
    plan[0, 0] += [lambda: tokens_start(0), lambda: tokens_start(1)]
    plan[0, 1] += [lambda: [p_copy(k).start() for k in range(1, NMP)], own_rows]
    plan[0, 3] += [lambda: tokens_x(0)]
    plan[0, 6] += [lambda: tokens_on(0), lambda: tokens_x(1)]
    plan[1, 1] += [lambda: tokens_last(0)]
    plan[1, 2] += [lambda: ring_finish(0), lambda: tokens_done(0)]
    for j, u in enumerate(units(0)):
        plan[1, 2 + j] += [u]
    plan[1, 4] += [lambda: tokens_on(1)]
    plan[1, 6] += [lambda: tokens_last(1)]
    plan[2, 2] += [lambda: unit_sum(0), lambda: ring_finish(1)]
    for j, u in enumerate(units(1)):
        plan[2, 2 + j] += [u]
    plan[3, 2] += [lambda: unit_sum(1), lambda: ring_finish(2), lambda: tokens_done(1)]
    for j, u in enumerate(units(2)):
        plan[3, 2 + j] += [u]

    for p in range(4):
        for i in range(7):
            ring_issue(p, i)
            for u in plan[p, i]:
                u()
    ring_finish(3)
    for u in units(3):
        u()
    unit_sum(2)
    unit_sum(3)
    p_all[m] = ps[...]
    for k in range(1, NMP):
        p_copy(k).wait_recv()
    p_out[...] = jnp.sum(p_all[...], axis=0)

    for p in range(4):
        for way in range(2):
            for i in range(7):
                ring_copy(p, way, i).wait_send()
            half_copy(p, way).wait_send()
            for h in range(2):
                full_copy(p, way, h).wait_send()
    for a in range(2):
        for k in (1, 2, 3):
            y_copy(a, k).wait_send()
        for i in range(4):
            x_copy(a, i).wait_send()
        for i in range(5):
            core_copy(a, i).wait_send()
    for k in range(1, NMP):
        p_copy(k).wait_send()


def products(at, wb, ps):
    vmem = pl.BlockSpec(memory_space=pltpu.VMEM)
    dma = pltpu.SemaphoreType.DMA
    return pl.pallas_call(
        products_kernel,
        out_shape=(jax.ShapeDtypeStruct((3, SEQ, WIDE), F32), jax.ShapeDtypeStruct((8, SEQ), F32)),
        in_specs=[vmem] * 3,
        out_specs=(vmem, vmem),
        scratch_shapes=[
            pltpu.VMEM((NY, 2, KLEN, SEQ), BF),
            pltpu.VMEM((3, KLEN, WIDE), BF),
            pltpu.VMEM((3, 2, 128, WIDE), BF),
            pltpu.VMEM((3, 2, SEQ, WIDE), BF),
            pltpu.VMEM((3, 2, 128, WIDE), BF),
            pltpu.VMEM((3, 2, SEQ, WIDE), BF),
            pltpu.VMEM((NMP, 8, SEQ), F32),
            dma((4, 2, 7)),
            dma((4, 2, 7)),
            dma((2, 3)),
            dma((2, 3)),
            dma((2,)),
            dma((2, 4)),
            dma((2, 4)),
            dma((2, 5)),
            dma((2, 5)),
            dma((4, 2)),
            dma((4, 2)),
            dma((4, 2, 2)),
            dma((4, 2, 2)),
            dma((NMP - 1,)),
            dma((NMP - 1,)),
        ],
        compiler_params=pltpu.CompilerParams(collective_id=0, has_side_effects=True),
        name="products",
    )(at, wb, ps)


def group_sum_kernel(v, out, land, ss, rs):
    d, m = lax.axis_index("dp"), lax.axis_index("mp")
    bar = pltpu.get_barrier_semaphore()
    for k in range(1, NMP):
        signal(bar, d, lax.rem(m + k, NMP))
    pl.semaphore_wait(bar, NMP - 1)

    def copy(k):
        return remote(v, land.at[m], ss.at[k - 1], rs.at[k - 1], d, lax.rem(m + k, NMP))

    for k in range(1, NMP):
        copy(k).start()
    land[m] = v[...]
    for k in range(1, NMP):
        copy(k).wait_recv()
    out[...] = jnp.sum(land[...], axis=0)
    for k in range(1, NMP):
        copy(k).wait_send()


def group_sum(v, cid):
    vmem = pl.BlockSpec(memory_space=pltpu.VMEM)
    dma = pltpu.SemaphoreType.DMA
    return pl.pallas_call(
        group_sum_kernel,
        out_shape=jax.ShapeDtypeStruct(v.shape, F32),
        in_specs=[vmem],
        out_specs=vmem,
        scratch_shapes=[pltpu.VMEM((NMP, *v.shape), F32), dma((NMP - 1,)), dma((NMP - 1,))],
        compiler_params=pltpu.CompilerParams(collective_id=cid, has_side_effects=True),
        name=f"group_sum_{cid}",
    )(v)


def final_kernel(u, s, u_out, s_out, u_land, s_land, us, ur, ss, sr):
    d, m = lax.axis_index("dp"), lax.axis_index("mp")
    z, y = d // NY, lax.rem(d, NY)
    bar = pltpu.get_barrier_semaphore()

    def greet(k, carry):
        signal(bar, lax.rem(d + k, NDP), m)
        return carry

    lax.fori_loop(1, NDP, greet, 0)

    def is_self(dd, mm):
        return jnp.logical_and(dd == d, mm == m)

    def greet_source(k, carry):
        @pl.when(jnp.logical_not(is_self(k, z)))
        def _():
            signal(bar, k, z)

        return carry

    lax.fori_loop(0, NDP, greet_source, 0)
    mine = (z == m).astype(jnp.int32)
    pl.semaphore_wait(bar, NDP - 1 + NDP - mine)

    def u_copy(k):
        yy, mm = k // NMP, lax.rem(k, NMP)
        dd = m * NY + yy
        return remote(u.at[yy], u_land.at[d], us.at[k], ur.at[d], dd, mm), is_self(dd, mm)

    def s_copy(k):
        dd = lax.rem(d + k, NDP)
        return remote(s.at[dd], s_land.at[d], ss.at[k], sr.at[d], dd, m)

    def u_start(k, carry):
        copy, own = u_copy(k)

        @pl.when(jnp.logical_not(own))
        def _():
            copy.start()

        return carry

    def s_start(k, carry):
        s_copy(k).start()
        return carry

    lax.fori_loop(0, NDP, u_start, 0)
    lax.fori_loop(1, NDP, s_start, 0)
    s_land[d] = s[d]

    @pl.when(z == m)
    def _():
        u_land[d] = u[y]

    def u_wait(k, carry):
        @pl.when(jnp.logical_not(is_self(k, z)))
        def _():
            remote(u.at[0], u_land.at[k], us.at[0], ur.at[k], d, m).wait_recv()

        return carry

    def s_wait(k, carry):
        dd = lax.rem(d + k, NDP)
        remote(s.at[0], s_land.at[dd], ss.at[0], sr.at[dd], d, m).wait_recv()
        return carry

    lax.fori_loop(0, NDP, u_wait, 0)
    lax.fori_loop(1, NDP, s_wait, 0)
    u_out[...] = jnp.sum(u_land[...].astype(F32), axis=0)
    s_out[...] = jnp.sum(s_land[...], axis=0)

    def sent(k, carry):
        copy, own = u_copy(k)

        @pl.when(jnp.logical_not(own))
        def _():
            copy.wait_send()

        return carry

    def s_sent(k, carry):
        s_copy(k).wait_send()
        return carry

    lax.fori_loop(0, NDP, sent, 0)
    lax.fori_loop(1, NDP, s_sent, 0)


def final_sums(u, s):
    vmem = pl.BlockSpec(memory_space=pltpu.VMEM)
    dma = pltpu.SemaphoreType.DMA
    return pl.pallas_call(
        final_kernel,
        out_shape=(jax.ShapeDtypeStruct(u.shape[1:], F32), jax.ShapeDtypeStruct(s.shape[1:], F32)),
        in_specs=[vmem, vmem],
        out_specs=(vmem, vmem),
        scratch_shapes=[
            pltpu.VMEM((NDP, *u.shape[1:]), u.dtype),
            pltpu.VMEM(s.shape, s.dtype),
            dma((NDP,)),
            dma((NDP,)),
            dma((NDP,)),
            dma((NDP,)),
        ],
        compiler_params=pltpu.CompilerParams(collective_id=3, has_side_effects=True),
        name="final_sums",
    )(u, s)


def per_device(
    residual_input,
    cotangent,
    lengths,
    norm_gain_vector,
    gate_projection_weight,
    up_projection_weight,
    down_projection_weight,
    up_adapter_first,
    up_adapter_second,
    down_adapter_first,
    down_adapter_second,
):
    clip_limit = clip_coefficient * math.sqrt(2.0 * ADAPTER_RANK * (MODEL_WIDTH + HIDDEN_SHARD))
    d, m = lax.axis_index("dp"), lax.axis_index("mp")
    features = residual_input.shape[1]
    gain = lax.dynamic_slice(norm_gain_vector, (m * features,), (features,)).astype(F32)[None, :]
    positions = lax.broadcasted_iota(jnp.int32, (SEQ, 1), 0)
    live = (positions < lengths[0]).astype(F32)
    output_gradient = (cotangent.astype(F32) * live).astype(BF)
    wide = residual_input.astype(F32)
    scaled = (wide * gain).astype(BF)
    at = jnp.stack([scaled.T.reshape(NY, ROWS, SEQ), output_gradient.T.reshape(NY, ROWS, SEQ)], axis=1)
    ps = jnp.broadcast_to(jnp.sum(wide * wide, axis=1)[None, :], (8, SEQ))
    first = lax.dynamic_slice(up_adapter_first, (d * ROWS, 0), (ROWS, ADAPTER_RANK))
    second = lax.dynamic_slice(down_adapter_second, (0, d * ROWS), (ADAPTER_RANK, ROWS)).T
    rest = jnp.zeros((ROWS, WIDE - COLS - ADAPTER_RANK), BF)
    wb = jnp.stack(
        [
            jnp.concatenate([gate_projection_weight, jnp.zeros_like(first), rest], axis=1),
            jnp.concatenate([up_projection_weight, first, rest], axis=1),
            jnp.concatenate([down_projection_weight, second, rest], axis=1),
        ]
    )
    c_all, squares_of_rows = products(at, wb, ps)
    inverse = lax.rsqrt(squares_of_rows[0] * (1.0 / MODEL_WIDTH) + norm_eps)[:, None]
    gate = c_all[0, :, :COLS] * inverse
    up_frozen_output = c_all[1, :, :COLS] * inverse
    up_adapter_latent = (c_all[1, :, COLS : COLS + ADAPTER_RANK] * inverse).astype(BF)
    backward_frozen = c_all[2, :, :COLS]
    backward_adapter = c_all[2, :, COLS : COLS + ADAPTER_RANK].astype(BF)

    up_activation = up_frozen_output + adapter_scale * jnp.dot(
        up_adapter_latent, up_adapter_second, preferred_element_type=F32
    )
    gate_act = jax.nn.silu(gate)
    hidden_activation = (gate_act * up_activation).astype(BF)
    hidden_gradient = backward_frozen + adapter_scale * contract_columns(backward_adapter, down_adapter_first)
    up_gradient = (hidden_gradient * gate_act).astype(BF)
    down_partial = lax.dot_general(
        down_adapter_first, hidden_activation, (((0,), (1,)), ((), ())), preferred_element_type=F32
    )
    up_partial = contract_columns(up_adapter_second, up_gradient)
    down_first_gradient = adapter_scale * contract_row_dims(hidden_activation, backward_adapter)
    up_second_gradient = adapter_scale * contract_row_dims(up_gradient, up_adapter_latent)
    shared = jnp.sum(down_first_gradient * down_first_gradient) + jnp.sum(up_second_gradient * up_second_gradient)
    latents = group_sum(
        jnp.concatenate([down_partial, up_partial, jnp.broadcast_to(shared, (8, SEQ))], axis=0), 1
    )
    down_adapter_latent = latents[:ADAPTER_RANK].astype(BF)
    up_adapter_hidden = latents[ADAPTER_RANK : 2 * ADAPTER_RANK].astype(BF)
    normalized = (wide * inverse * gain).astype(BF)
    up_first_gradient = adapter_scale * lax.dot_general(
        normalized, up_adapter_hidden, (((0,), (1,)), ((), ())), preferred_element_type=F32
    )
    down_second_gradient = adapter_scale * lax.dot_general(
        output_gradient, down_adapter_latent, (((0,), (1,)), ((), ())), preferred_element_type=F32
    )
    owned = jnp.sum(up_first_gradient * up_first_gradient) + jnp.sum(down_second_gradient * down_second_gradient)
    owned_total = group_sum(jnp.broadcast_to(owned, (8, 128)), 2)[0, 0]
    factor = jnp.minimum(1.0, clip_limit / (jnp.sqrt(owned_total + latents[2 * ADAPTER_RANK, 0]) + 1e-06))
    u = (factor * jnp.concatenate([up_first_gradient, down_second_gradient], axis=1)).astype(BF)
    u = u.reshape(NY, ROWS * 2 * ADAPTER_RANK // 128, 128)
    s = factor * jnp.concatenate([down_first_gradient, up_second_gradient], axis=1)
    s = jnp.pad(s.reshape(NDP, COLS), ((0, 0), (0, 1024 - COLS))).reshape(NDP, 8, 128)
    u_sum, s_sum = final_sums(u, s)
    u_sum = u_sum.reshape(ROWS, 2 * ADAPTER_RANK)
    s_sum = s_sum.reshape(1024)[:COLS].reshape(COLS // NDP, 2 * ADAPTER_RANK)
    return (
        u_sum[:, :ADAPTER_RANK],
        s_sum[:, ADAPTER_RANK:].T,
        s_sum[:, :ADAPTER_RANK],
        u_sum[:, ADAPTER_RANK:].T,
    )


def solution(mesh):
    return jax.shard_map(
        per_device,
        mesh=mesh,
        in_specs=(
            P("dp", "mp"),
            P("dp", "mp"),
            P("dp"),
            P(),
            P("dp", "mp"),
            P("dp", "mp"),
            P("dp", "mp"),
            P(),
            P(None, "mp"),
            P("mp", None),
            P(),
        ),
        out_specs=(P("dp", None), P(None, ("mp", "dp")), P(("mp", "dp"), None), P(None, "dp")),
        check_vma=False,
    )
```

time: 396 us -> 189 us (0.48)
  waiting for transfers between devices: 276 us -> 0 us
  Pallas kernels: 0 us -> 153 us
  matrix products: 39.5 us -> 9.8 us
  blocking collectives: 22.9 us -> 0 us
  starting transfers between devices: 18 us -> 0 us
  between operations: 18.3 us -> 5.54 us
  other arithmetic: 12.1 us -> 7.3 us
    all_gather x2 -> x0, waiting for transfers between devices: 232 us -> none  [side_by_side(): lax.all_gather(both, axis, axis=dim, tiled=True)]
    pallas_call x0 -> x4, Pallas kernels: none -> 153 us  [the longest x1 99.1 us: products(): pl.pallas_call(products_kernel, out_shape=(jax.ShapeDtypeStruct((3, SEQ,...]
    all_to_all x4 -> x0, waiting for transfers between devices: 44 us -> none  [sent_and_summed(): lax.all_to_all(parts, axis, split_axis=0, concat_axis=0, tiled=True)]
    dot_general x6 -> x4, matrix products: 32.3 us -> 3.89 us  [the longest x1 1.99 us: per_device(): jnp.dot(up_adapter_latent, up_adapter_second, preferred_element_type=F32)]
    psum x1 -> x0, blocking collectives: 22.9 us -> none  [per_device(): up_summed, shared_total = lax.psum((up_partial_output, shared), 'mp')]
    all_to_all x4 -> x0, starting transfers between devices: 17.9 us -> none  [sent_and_summed(): lax.all_to_all(parts, axis, split_axis=0, concat_axis=0, tiled=True)]
  transfers between devices with their start and end apart: 6 -> 0, of which waited for: 6 -> 0; matrix products, arithmetic and copies ran while one was open for 5% -> 0% of each run, Pallas kernels for 0% -> 0%
where the time goes in v1:
time: 189 us; the launch traced here: 187 us
  Pallas kernels  153 us (81%)
  local copies, waits for them, and re-layouts  11.7 us (6%)
  matrix products  9.8 us (5%)
  other arithmetic  7.3 us (4%)
  between operations  5.54 us (3%)
    pallas_call x1, Pallas kernels, products(): pl.pallas_call(products_kernel, out_shape=(jax.ShapeDtypeStruct((3, SEQ,...  99.1 us
    pallas_call x1, Pallas kernels, final_sums(): pl.pallas_call(final_kernel, out_shape=(jax.ShapeDtypeStruct(u.shape[1:],...  36.8 us
    pallas_call x2, Pallas kernels, group_sum(): pl.pallas_call(group_sum_kernel, out_shape=jax.ShapeDtypeStruct(v.shape,...  17.2 us

profile of v1, /device:TPU:6, one launch (start us, length us, event | category | flops | bytes accessed | tf_op | source)
XLA Modules:
  0.0 187.4 jit_solution(1302326381680944056)
XLA Ops:
  1.5 0.8 dynamic-slice_convert_fusion
  2.4 0.8 constant_dynamic-slice_fusion
  3.4 1.1 fusion.14
  4.7 1.2 fusion.7
  6.6 0.9 pad_maximum_fusion.1.at
  7.7 1.0 pad_maximum_fusion.wb
  8.7 99.1 %products.1 = (f32[3,256,896]{2,1,0:T(8,128)}, f32[8,256]{1,0:T(8,128)}) custom-call(bf16[4,2,160,256]{3,2,1,0:T(8,128)(2,1)} %pad_maximum_fusion.1.at, bf16[3,160,896]{2,1,0:T(8,128)(2,1)} %pad_maximum_fusion.wb, f32[8,256]{1,0:T(8,128)} %broadcast_in_dim.18.ps), custom_call_target="tpu_custom_call" | custom-call | tf_op jit(solution)/shard_map/products/pallas_call | solution.py:297
  107.8 0.7 add_rsqrt_fusion
  108.5 2.0 %fusion.4 = bf16[256,864]{1,0:T(8,128)(2,1)S(1)} fusion(bf16[16,864]{1,0:T(8,128)(2,1)S(1)} %copy-done.7, f32[3,256,896]{2,1,0:T(8,128)} %get-tuple-element.9, f32[256]{0:T(256)S(1)} %bitcast.68), kind=kOutput, calls=%fused_computation.6 | convolution fusion | flops 9297920 | bytes 2439168 | tf_op jit(solution)/shard_map/dot_general | solution.py:517
  110.7 1.9 multiply_reduce_fusion.1
  112.6 2.0 %fusion.5 = bf16[256,864]{1,0:T(8,128)(2,1)S(1)} fusion(bf16[864,16]{0,1:T(8,128)(2,1)S(1)} %copy-done.6, f32[3,256,896]{2,1,0:T(8,128)} %get-tuple-element.9, f32[256]{0:T(256)S(1)} %bitcast.69), kind=kOutput, calls=%fused_computation.7 | convolution fusion | flops 9072640 | bytes 2437120 | tf_op jit(solution)/shard_map/dot_general | solution.py:39
  114.6 1.8 multiply_reduce_fusion
  118.1 0.7 maximum_maximum_fusion.v
  118.8 9.4 %group_sum_1.1 = f32[40,256]{1,0:T(8,128)} custom-call(f32[40,256]{1,0:T(8,128)} %maximum_maximum_fusion.v), custom_call_target="tpu_custom_call" | custom-call | tf_op jit(solution)/shard_map/group_sum_1/pallas_call | solution.py:354
  128.2 1.2 slice.60
  129.4 0.8 convert.8
  130.1 0.9 multiply_reduce_fusion.3
  131.0 0.8 multiply_reduce_fusion.2
  133.8 7.8 %group_sum_2.1 = f32[8,128]{1,0:T(8,128)} custom-call(f32[8,128]{1,0:T(8,128)} %broadcast_in_dim.20.v), custom_call_target="tpu_custom_call" | custom-call | tf_op jit(solution)/shard_map/group_sum_2/pallas_call | solution.py:354
  141.6 1.2 slice.59
  144.3 0.8 convert_element_type.62.u
  146.1 36.8 %final_sums.1 = (f32[40,128]{1,0:T(8,128)}, f32[8,128]{1,0:T(8,128)}) custom-call(bf16[4,40,128]{2,1,0:T(8,128)(2,1)} %convert_element_type.62.u, f32[32,8,128]{2,1,0:T(8,128)} %bitcast.65), custom_call_target="tpu_custom_call" | custom-call | tf_op jit(solution)/shard_map/final_sums/pallas_call | solution.py:457
  182.9 0.8 slice.62
  185.1 0.8 reshape.56
  (44 shorter events, 6.7 us)
Async XLA Ops:
  0.6 1.6 copy-start
  0.6 6.8 %copy-start.4 = (bf16[160,864]{1,0:T(8,128)(2,1)S(1)}, bf16[160,864]{1,0:T(8,128)(2,1)}, u32[]{:S(2)}) copy-start(bf16[160,864]{1,0:T(8,128)(2,1)} %param.17) | copy-start | bytes 829444
  0.7 6.8 %copy-start.3 = (bf16[160,864]{1,0:T(8,128)(2,1)S(1)}, bf16[160,864]{1,0:T(8,128)(2,1)}, u32[]{:S(2)}) copy-start(bf16[160,864]{1,0:T(8,128)(2,1)} %param.16) | copy-start | bytes 829444
  0.7 6.8 %copy-start.5 = (bf16[160,864]{1,0:T(8,128)(2,1)S(1)}, bf16[160,864]{1,0:T(8,128)(2,1)}, u32[]{:S(2)}) copy-start(bf16[160,864]{1,0:T(8,128)(2,1)} %param.15) | copy-start | bytes 829444
  7.5 101.0 %copy-start.7 = (bf16[16,864]{1,0:T(8,128)(2,1)S(1)}, bf16[16,864]{1,0:T(8,128)(2,1)}, u32[]{:S(2)}) copy-start(bf16[16,864]{1,0:T(8,128)(2,1)} %param.19) | copy-start | bytes 82948
  108.5 2.0 %copy-start.6 = (bf16[864,16]{0,1:T(8,128)(2,1)S(1)}, bf16[864,16]{0,1:T(8,128)(2,1)}, u32[]{:S(2)}) copy-start(bf16[864,16]{0,1:T(8,128)(2,1)} %param.20) | copy-start | bytes 82948
  112.6 17.6 %copy-start.2 = (bf16[256,640]{1,0:T(8,128)(2,1)S(1)}, bf16[256,640]{1,0:T(8,128)(2,1)}, u32[]{:S(2)}) copy-start(bf16[256,640]{1,0:T(8,128)(2,1)} %param.11) | copy-start | bytes 983044
  112.6 18.4 %copy-start.1 = (bf16[256,640]{1,0:T(8,128)(2,1)S(1)}, bf16[256,640]{1,0:T(8,128)(2,1)}, u32[]{:S(2)}) copy-start(bf16[256,640]{1,0:T(8,128)(2,1)} %param.12) | copy-start | bytes 983044

commit v2 on v1

v2 whole, which is shorter than its diff:
```python
import math

import jax
import jax.numpy as jnp
from jax import lax
from jax.experimental import pallas as pl
from jax.experimental.pallas import tpu as pltpu
from jax.sharding import PartitionSpec as P

MODEL_WIDTH = 5120
HIDDEN_SHARD = 6912
ADAPTER_RANK = 16

norm_eps = 1e-06
adapter_scale = 2.0
clip_coefficient = 0.005

NZ, NY, NX, NC = 8, 4, 4, 2
NMP = NX * NC
NDP = NZ * NY
ROWS = 160
KLEN = ROWS * NZ
SEQ = 256
COLS = 864
WIDE = 896
HALF = ROWS // 2

PIECES = ((0, 0, 0, 896), (1, 0, 0, 896), (2, 1, 384, 512), (2, 1, 0, 384))
RING = (((0, 0), (0, 1), (1, 0), (1, 1), (2, 0), (2, 1), (3, 0)), ((0, 0), (0, 1), (1, 0), (1, 1), (2, 0), (2, 1), (3, 1)))
ORDER = (
    *((0, i) for i in range(7)), *((1, i) for i in range(7)),
    (2, 0), (2, 1), (2, 2), (2, 3), (3, 0), (3, 1), (2, 4), (2, 5), (3, 2), (3, 3), (2, 6), (3, 4), (3, 5), (3, 6),
)
LANE0 = 768
SPOT = COLS - LANE0
FEATS = MODEL_WIDTH // NMP
SHARE = COLS // NDP
MESH = pl.DeviceIdType.MESH
BF, F32 = jnp.bfloat16, jnp.float32


def contract_row_dims(left, right):
    return lax.dot_general(left, right, (((0,), (0,)), ((), ())), preferred_element_type=F32)


def contract_columns(left, right):
    return lax.dot_general(left, right, (((1,), (1,)), ((), ())), preferred_element_type=F32)


def remote(src, dst, send, recv, dp, mp):
    return pltpu.make_async_remote_copy(
        src_ref=src, dst_ref=dst, send_sem=send, recv_sem=recv, device_id={"dp": dp, "mp": mp}, device_id_type=MESH
    )


def signal(sem, dp, mp):
    pl.semaphore_signal(sem, inc=1, device_id={"dp": dp, "mp": mp}, device_id_type=MESH)


def gradients_kernel(
    lengths, xin, gin, gain, wg, wu, wd, adp, ad, u_out, s_out,
    c, at, wb, xt, a_all, b_all, cs2, cs1, near, cr2, cr1, ps, p_all, lat, hid, full, v, v_all, q, q_all, part, msg, msg_all, us, u_row,
    bs, br, ays, ayr, loc, axs, axr, ads, adr, c2s, c2r, c1s, c1r, pss, psr, vs, vr, qs, qr, ms, mr, us4, ur4,
):
    d, m = lax.axis_index("dp"), lax.axis_index("mp")
    z, y, x, core = d // NY, lax.rem(d, NY), m // NC, lax.rem(m, NC)

    def dp_of(zz, yy):
        return lax.rem(zz, NZ) * NY + lax.rem(yy, NY)

    def mp_of(xx, cc):
        return lax.rem(xx, NX) * NC + cc

    up_z, down_z = dp_of(z + 1, y), dp_of(z + NZ - 1, y)
    up_y, down_y = dp_of(z, y + 1), dp_of(z, y + NY - 1)
    up_x, down_x = mp_of(x + 1, core), mp_of(x + NX - 1, core)
    far_x = mp_of(x + 2, core)
    twin = mp_of(x, 1 - core)

    bar = pltpu.get_barrier_semaphore()
    signal(bar, up_z, m)
    signal(bar, down_z, m)
    for k in range(1, NY):
        signal(bar, dp_of(z, y + k), m)
    for k in range(1, NMP):
        signal(bar, d, lax.rem(m + k, NMP))

    def assemble(w, ref):
        wb[w, :, :COLS] = ref[...]
        tile = wb[w, :, LANE0:]
        lane = lax.broadcasted_iota(jnp.int32, tile.shape, 1)
        wb[w, :, LANE0:] = jnp.where(lane < SPOT, tile, adp[w])

    assemble(0, wg)
    pl.semaphore_wait(bar, 2 + NY - 1 + NMP - 1)

    def rows_of(zz, h, n):
        return pl.ds(pl.multiple_of(zz * ROWS + h * HALF, 16), n)

    def ring_copy(p, way, i):
        w, _, c0, n = PIECES[p]
        s, h = RING[way][i]
        src_z = lax.rem(z + (NZ - s if way == 0 else s), NZ)
        cols = pl.ds(c0, n)
        here = wb.at[w, pl.ds(h * HALF, HALF), cols] if s == 0 else b_all.at[w, rows_of(src_z, h, HALF), cols]
        there = b_all.at[w, rows_of(src_z, h, HALF), cols]
        return remote(here, there, bs.at[p, way, i], br.at[p, way, i], up_z if way == 0 else down_z, m)

    def ring_issue(p, i):
        for way in range(2):
            s, h = RING[way][i]
            if s:
                ring_copy(p, way, 2 * (s - 1) + h).wait_recv()
            ring_copy(p, way, i).start()

    def ring_finish(p):
        for way in range(2):
            for i in (5, 6) if way == 0 else (4, 6):
                ring_copy(p, way, i).wait_recv()

    def feats(mm):
        return pl.ds(pl.multiple_of(mm * ROWS, 16), ROWS)

    def y_copy(a, k):
        yy = lax.rem(y + k, NY)
        return remote(at.at[yy, a], a_all.at[y, a, feats(m), :], ays.at[a, k - 1], ayr.at[a, k - 1], dp_of(z, yy), m)

    def own_copy(a):
        return pltpu.make_async_copy(at.at[y, a], a_all.at[y, a, feats(m), :], loc.at[a])

    def block(a, mm, e0, ne):
        return a_all.at[pl.ds(e0, ne), a, feats(mm), :]

    def x_copy(a, i):
        mm, e0, ne, to = ((m, 0, 4, up_x), (m, 0, 4, down_x), (down_x, 0, 2, up_x), (up_x, 2, 2, down_x))[i]
        return remote(block(a, mm, e0, ne), block(a, mm, e0, ne), axs.at[a, i], axr.at[a, i], d, to)

    def core_copy(a, i):
        mm, e0, ne = ((m, 0, 4), (down_x, 0, 4), (up_x, 0, 4), (far_x, 0, 2), (far_x, 2, 2))[i]
        return remote(block(a, mm, e0, ne), block(a, mm, e0, ne), ads.at[a, i], adr.at[a, i], d, twin)

    def tokens_start(a):
        for k in (2, 1, 3):
            y_copy(a, k).start()
        own_copy(a).start()

    def tokens_x(a):
        own_copy(a).wait()
        for k in (1, 2, 3):
            y_copy(a, k).wait_recv()
        x_copy(a, 0).start()
        x_copy(a, 1).start()
        core_copy(a, 0).start()

    def tokens_on(a):
        x_copy(a, 0).wait_recv()
        x_copy(a, 2).start()
        x_copy(a, 1).wait_recv()
        x_copy(a, 3).start()
        core_copy(a, 1).start()
        core_copy(a, 2).start()

    def tokens_last(a):
        x_copy(a, 2).wait_recv()
        core_copy(a, 3).start()
        x_copy(a, 3).wait_recv()
        core_copy(a, 4).start()

    def tokens_done(a):
        for i in range(5):
            core_copy(a, i).wait_recv()

    def product(p, t, store):
        w, a, c0, n = PIECES[p]

        def tile(lo, size):
            acc = lax.dot_general(
                a_all[t, a], b_all[w, :, pl.ds(lo, size)], (((0,), (0,)), ((), ())), preferred_element_type=F32
            )
            store(w, lo, size, acc)

        def step(i, carry):
            tile(pl.multiple_of(c0 + i * 256, 128), 256)
            return carry

        lax.fori_loop(0, n // 256, step, 0)
        if n % 256:
            tile(c0 + n - n % 256, n % 256)

    def half_copy(p, way):
        w, _, c0, n = PIECES[p]
        cols = pl.ds(c0, n)
        return remote(
            cs2.at[w, way, :, cols], cr2.at[w, way, :, cols], c2s.at[p, way], c2r.at[p, way], up_y if way == 0 else down_y, m
        )

    def full_copy(p, way, h):
        w, _, c0, n = PIECES[p]
        part = (way, pl.ds(h * 128, 128), pl.ds(c0, n))
        return remote(
            cs1.at[(w, *part)], cr1.at[(w, *part)], c1s.at[p, way, h], c1r.at[p, way, h], up_y if way == 0 else down_y, m
        )

    def unit_far(p):
        def store(w, lo, size, acc):
            v = acc.astype(BF)
            cs2[w, 0, :, pl.ds(lo, size)] = v[:128]
            cs2[w, 1, :, pl.ds(lo, size)] = v[128:]

        product(p, lax.rem(y + 2, NY), store)
        half_copy(p, 0).start()
        half_copy(p, 1).start()

    def unit_near(p, way):
        def store(w, lo, size, acc):
            sent, kept = (acc[128:], acc[:128]) if way == 0 else (acc[:128], acc[128:])
            cs1[w, way, pl.ds((1 - way) * 128, 128), pl.ds(lo, size)] = sent.astype(BF)
            near[w, way, :, pl.ds(lo, size)] = kept

        product(p, lax.rem(y + (1 if way == 0 else NY - 1), NY), store)
        full_copy(p, way, 1 - way).start()

    def unit_pass(p):
        w, _, c0, n = PIECES[p]
        for way in range(2):
            half_copy(p, way).wait_recv()
            at_rows, cols = pl.ds(way * 128, 128), pl.ds(c0, n)
            total = near[w, way, :, cols] + cr2[w, way, :, cols].astype(F32)
            cs1[w, way, at_rows, cols] = total.astype(BF)
            full_copy(p, way, way).start()

    def unit_own(p):
        def store(w, lo, size, acc):
            c[w, :, pl.ds(lo, size)] = acc

        product(p, y, store)

    def unit_sum(p):
        w, _, c0, n = PIECES[p]
        cols = pl.ds(c0, n)
        for way in range(2):
            for h in range(2):
                full_copy(p, way, h).wait_recv()
        c[w, :, cols] += cr1[w, 0, :, cols].astype(F32) + cr1[w, 1, :, cols].astype(F32)

    def p_copy(k):
        return remote(ps, p_all.at[m], pss.at[k - 1], psr.at[k - 1], d, lax.rem(m + k, NMP))

    def own_rows():
        for w in range(3):
            b_all[w, rows_of(z, 0, ROWS), :] = wb[w]

    def normalize():
        p_all[m] = ps[...]
        for k in range(1, NMP):
            p_copy(k).wait_recv()
        inverse = lax.rsqrt(jnp.sum(p_all[...], axis=0)[:1] * (1.0 / MODEL_WIDTH) + norm_eps)
        gains = gain[...].astype(F32).T
        lane = lax.broadcasted_iota(jnp.int32, gains.shape, 1)
        column = jnp.sum(jnp.where(lane == m, gains, 0.0), axis=1, keepdims=True)
        normed = (xt[...] * inverse * column).astype(BF)
        for yy in range(NY):
            at[yy, 0] = normed[yy * ROWS : (yy + 1) * ROWS]

    def mask():
        token = lax.broadcasted_iota(jnp.int32, (1, SEQ), 1)
        live = (token < lengths[0]).astype(F32)
        masked = (gin[...].astype(F32).T * live).astype(BF)
        for yy in range(NY):
            at[yy, 1] = masked[yy * ROWS : (yy + 1) * ROWS]

    def rest():
        xt[...] = xin[...].astype(F32).T
        ps[...] = jnp.broadcast_to(jnp.sum(xt[...] * xt[...], axis=0, keepdims=True), ps.shape)
        for k in range(1, NMP):
            p_copy(k).start()
        assemble(1, wu)
        normalize()
        tokens_start(0)
        mask()
        tokens_start(1)
        assemble(2, wd)
        own_rows()

    def tile_of(i):
        return pl.ds(pl.multiple_of(i * 128, 128), 128)

    def spots(a):
        return a[SPOT : SPOT + ADAPTER_RANK]

    def forward_side():
        up_latent = c[1, :, LANE0:].astype(BF)
        lat[...] = jnp.zeros_like(lat)

        def chunk(i, carry):
            cols = tile_of(i)
            gate_act = jax.nn.silu(c[0, :, cols])
            c[0, :, cols] = gate_act
            up = c[1, :, cols] + adapter_scale * jnp.dot(up_latent, ad[0, :, cols], preferred_element_type=F32)
            hidden = (gate_act * up).astype(BF)
            hid[:, cols] = hidden
            lat[0] += contract_columns(ad[1, :, cols], hidden)
            return carry

        lax.fori_loop(0, WIDE // 128, chunk, 0)
        v[0] = spots(lat[0]).astype(BF)
        for k in range(1, NMP):
            v_copy(0, k).start()

    def down_side():
        v_all[0, m] = v[0]
        for k in range(1, NMP):
            v_copy(0, k).wait_recv()
        latent = jnp.sum(v_all[0].astype(F32), axis=0).astype(BF)
        for yy in range(NY):
            put(yy, 4, adapter_scale * contract_columns(latent, at[yy, 1]))

    def backward_side(lo, hi):
        up_latent = c[1, :, LANE0:].astype(BF)
        back_latent = c[2, :, LANE0:].astype(BF)

        def chunk(i, carry):
            cols = tile_of(i)
            back = c[2, :, cols] + adapter_scale * jnp.dot(back_latent, ad[1, :, cols], preferred_element_type=F32)
            up_gradient = (back * c[0, :, cols]).astype(BF)
            lat[1] += contract_columns(ad[0, :, cols], up_gradient)
            full[:ADAPTER_RANK, cols] = adapter_scale * spots(contract_row_dims(back_latent, hid[:, cols]))
            full[ADAPTER_RANK:, cols] = adapter_scale * spots(contract_row_dims(up_latent, up_gradient))
            return carry

        lax.fori_loop(lo, hi, chunk, 0)

    def v_copy(i, k):
        return remote(v.at[i], v_all.at[i, m], vs.at[i, k - 1], vr.at[i, k - 1], d, lax.rem(m + k, NMP))

    def q_copy(k):
        return remote(q, q_all.at[m], qs.at[k - 1], qr.at[k - 1], d, lax.rem(m + k, NMP))

    def put(yy, j0, rows):
        for j in range(4):
            part[(j0 + j) * NY + yy, 8:12] = rows[4 * j : 4 * j + 4, :128]
            part[(j0 + j) * NY + yy, 12:16, : ROWS - 128] = rows[4 * j : 4 * j + 4, 128:]

    plan = {
        1: [rest],
        3: [lambda: tokens_x(0)],
        6: [lambda: tokens_on(0), lambda: tokens_x(1)],
        8: [lambda: tokens_last(0)],
        9: [lambda: ring_finish(0), lambda: tokens_done(0), lambda: unit_far(0)],
        10: [lambda: unit_near(0, 0)],
        11: [lambda: unit_near(0, 1)],
        12: [lambda: tokens_on(1), lambda: unit_pass(0)],
        13: [lambda: unit_own(0)],
        15: [lambda: tokens_last(1)],
        16: [lambda: ring_finish(1), lambda: unit_far(1)],
        17: [lambda: unit_near(1, 0)],
        18: [lambda: unit_near(1, 1)],
        19: [lambda: unit_sum(0)],
        20: [lambda: unit_pass(1)],
        21: [lambda: unit_own(1), lambda: tokens_done(1)],
        27: [lambda: ring_finish(2), lambda: unit_far(2), lambda: unit_near(2, 0), lambda: unit_near(2, 1)],
    }
    part[...] = jnp.zeros_like(part)
    for at_position, (p, i) in enumerate(ORDER):
        ring_issue(p, i)
        for u in plan.get(at_position, ()):
            u()
    ring_finish(3)
    unit_far(3)
    unit_near(3, 0)
    unit_near(3, 1)
    unit_pass(2)
    unit_own(2)
    unit_sum(1)
    forward_side()
    unit_pass(3)
    unit_own(3)
    down_side()
    unit_sum(2)
    backward_side(3, WIDE // 128)
    unit_sum(3)
    backward_side(0, 3)
    v[1] = spots(lat[1]).astype(BF)
    for k in range(1, NMP):
        v_copy(1, k).start()
    v_all[1, m] = v[1]

    for i in range(NDP):
        for r in range(4):
            part[i, :8, r * 32 : r * 32 + 32] = full[r * 8 : r * 8 + 8, i * SHARE : i * SHARE + 32]
    squares = jnp.sum(full[...] * full[...], keepdims=True)
    for k in range(1, NMP):
        v_copy(1, k).wait_recv()
    latent = jnp.sum(v_all[1].astype(F32), axis=0).astype(BF)
    for yy in range(NY):
        put(yy, 0, adapter_scale * contract_columns(latent, at[yy, 0]))
    features = part[:, 8:, :]
    squares = squares + jnp.sum(jnp.sum(features * features, axis=0), keepdims=True)
    q[...] = jnp.broadcast_to(squares, q.shape)
    for k in range(1, NMP):
        q_copy(k).start()
    q_all[m] = q[...]
    for k in range(1, NMP):
        q_copy(k).wait_recv()
    clip_limit = clip_coefficient * math.sqrt(2.0 * ADAPTER_RANK * (MODEL_WIDTH + HIDDEN_SHARD))
    norm = jnp.sqrt(jnp.sum(q_all[...], axis=0))
    factor = jnp.minimum(1.0, clip_limit / (norm + 1e-06))[:1, :1]
    msg[...] = (part[...] * factor[None]).astype(BF)

    def m_copy(k):
        dd = lax.rem(d + k, NDP)
        return remote(msg.at[dd], msg_all.at[d], ms.at[k], mr.at[d], dd, m)

    def m_start(k, carry):
        m_copy(k).start()
        return carry

    def m_arrive(k, carry):
        dd = lax.rem(d + k, NDP)
        remote(msg.at[0], msg_all.at[dd], ms.at[k], mr.at[dd], dd, m).wait_recv()
        return carry

    lax.fori_loop(1, NDP, m_start, 0)
    msg_all[d] = msg[d]
    lax.fori_loop(1, NDP, m_arrive, 0)
    summed = jnp.sum(msg_all[...].astype(F32), axis=0)
    us[...] = summed[8:]

    goal = m * NY + y
    here = z == m

    def u_copy(k):
        return remote(us, u_row.at[z], us4.at[k], ur4.at[z], goal, lax.rem(m + k, NMP))

    for k in range(1, NMP):
        u_copy(k).start()

    @pl.when(jnp.logical_not(here))
    def _():
        u_copy(0).start()

    @pl.when(here)
    def _():
        u_row[z] = us[...]

    for r in range(4):
        s_out[r * 8 : r * 8 + 8] = summed[:8, r * 32 : r * 32 + SHARE]

    for j in range(NZ):
        @pl.when(jnp.logical_not(jnp.logical_and(here, z == j)))
        def _():
            remote(us, u_row.at[j], us4.at[0], ur4.at[j], goal, lax.rem(m + 1, NMP)).wait_recv()

        u_out[4 * j : 4 * j + 4, :128] = u_row[j, :4]
        u_out[4 * j : 4 * j + 4, 128:] = u_row[j, 4:, : ROWS - 128]

    def m_sent(k, carry):
        m_copy(k).wait_send()
        return carry

    lax.fori_loop(1, NDP, m_sent, 0)
    for k in range(1, NMP):
        v_copy(0, k).wait_send()
        v_copy(1, k).wait_send()
        q_copy(k).wait_send()
        u_copy(k).wait_send()

    @pl.when(jnp.logical_not(here))
    def _():
        u_copy(0).wait_send()

    for p in range(4):
        for way in range(2):
            for i in range(7):
                ring_copy(p, way, i).wait_send()
            half_copy(p, way).wait_send()
            for h in range(2):
                full_copy(p, way, h).wait_send()
    for a in range(2):
        for k in (1, 2, 3):
            y_copy(a, k).wait_send()
        for i in range(4):
            x_copy(a, i).wait_send()
        for i in range(5):
            core_copy(a, i).wait_send()
    for k in range(1, NMP):
        p_copy(k).wait_send()


def gradients(lengths, x, g, gain, wg, wu, wd, adp, ad):
    vmem = pl.BlockSpec(memory_space=pltpu.VMEM)
    dma = pltpu.SemaphoreType.DMA
    return pl.pallas_call(
        gradients_kernel,
        out_shape=(
            jax.ShapeDtypeStruct((2 * ADAPTER_RANK, ROWS), F32),
            jax.ShapeDtypeStruct((2 * ADAPTER_RANK, SHARE), F32),
        ),
        in_specs=[pl.BlockSpec(memory_space=pltpu.SMEM), *[vmem] * 8],
        out_specs=(vmem, vmem),
        scratch_shapes=[
            pltpu.VMEM((3, SEQ, WIDE), F32),
            pltpu.VMEM((NY, 2, ROWS, SEQ), BF),
            pltpu.VMEM((3, ROWS, WIDE), BF),
            pltpu.VMEM((FEATS, SEQ), F32),
            pltpu.VMEM((NY, 2, KLEN, SEQ), BF),
            pltpu.VMEM((3, KLEN, WIDE), BF),
            pltpu.VMEM((3, 2, 128, WIDE), BF),
            pltpu.VMEM((3, 2, SEQ, WIDE), BF),
            pltpu.VMEM((3, 2, 128, WIDE), F32),
            pltpu.VMEM((3, 2, 128, WIDE), BF),
            pltpu.VMEM((3, 2, SEQ, WIDE), BF),
            pltpu.VMEM((8, SEQ), F32),
            pltpu.VMEM((NMP, 8, SEQ), F32),
            pltpu.VMEM((2, 128, SEQ), F32),
            pltpu.VMEM((SEQ, WIDE), BF),
            pltpu.VMEM((2 * ADAPTER_RANK, WIDE), F32),
            pltpu.VMEM((2, ADAPTER_RANK, SEQ), BF),
            pltpu.VMEM((2, NMP, ADAPTER_RANK, SEQ), BF),
            pltpu.VMEM((8, 128), F32),
            pltpu.VMEM((NMP, 8, 128), F32),
            pltpu.VMEM((NDP, 16, 128), F32),
            pltpu.VMEM((NDP, 16, 128), BF),
            pltpu.VMEM((NDP, 16, 128), BF),
            pltpu.VMEM((8, 128), F32),
            pltpu.VMEM((NZ, 8, 128), F32),
            dma((4, 2, 7)),
            dma((4, 2, 7)),
            dma((2, 3)),
            dma((2, 3)),
            dma((2,)),
            dma((2, 4)),
            dma((2, 4)),
            dma((2, 5)),
            dma((2, 5)),
            dma((4, 2)),
            dma((4, 2)),
            dma((4, 2, 2)),
            dma((4, 2, 2)),
            dma((NMP - 1,)),
            dma((NMP - 1,)),
            dma((2, NMP - 1)),
            dma((2, NMP - 1)),
            dma((NMP - 1,)),
            dma((NMP - 1,)),
            dma((NDP,)),
            dma((NDP,)),
            dma((NMP,)),
            dma((NMP,)),
        ],
        compiler_params=pltpu.CompilerParams(collective_id=0, has_side_effects=True),
        name="gradients",
    )(lengths, x, g, gain, wg, wu, wd, adp, ad)


def per_device(
    residual_input,
    cotangent,
    lengths,
    norm_gain_vector,
    gate_projection_weight,
    up_projection_weight,
    down_projection_weight,
    up_adapter_first,
    up_adapter_second,
    down_adapter_first,
    down_adapter_second,
):
    d = lax.axis_index("dp")
    first = lax.dynamic_slice(up_adapter_first, (d * ROWS, 0), (ROWS, ADAPTER_RANK))
    second = lax.dynamic_slice(down_adapter_second, (0, d * ROWS), (ADAPTER_RANK, ROWS)).T
    adp = jnp.stack([jnp.zeros_like(first), first, second])
    adp = jnp.pad(adp, ((0, 0), (0, 0), (SPOT, 128 - SPOT - ADAPTER_RANK)))
    ad = jnp.stack([up_adapter_second, down_adapter_first.T])
    ad = jnp.pad(ad, ((0, 0), (SPOT, 128 - SPOT - ADAPTER_RANK), (0, WIDE - COLS)))
    u, s = gradients(
        lengths,
        residual_input,
        cotangent,
        norm_gain_vector.reshape(NMP, FEATS),
        gate_projection_weight,
        up_projection_weight,
        down_projection_weight,
        adp,
        ad,
    )
    return (u[:ADAPTER_RANK].T, s[ADAPTER_RANK:], s[:ADAPTER_RANK].T, u[ADAPTER_RANK:])


def solution(mesh):
    return jax.shard_map(
        per_device,
        mesh=mesh,
        in_specs=(
            P("dp", "mp"),
            P("dp", "mp"),
            P("dp"),
            P(),
            P("dp", "mp"),
            P("dp", "mp"),
            P("dp", "mp"),
            P(),
            P(None, "mp"),
            P("mp", None),
            P(),
        ),
        out_specs=(P("dp", None), P(None, ("mp", "dp")), P(("mp", "dp"), None), P(None, "dp")),
        check_vma=False,
    )
```

time: 189 us -> 128 us (0.68)
  Pallas kernels: 153 us -> 119 us
  matrix products: 9.8 us -> 0 us
  local copies, waits for them, and re-layouts: 11.7 us -> 5.22 us
  other arithmetic: 7.3 us -> 0.88 us
  between operations: 5.54 us -> 1.37 us
    pallas_call x4 -> x1, Pallas kernels: 153 us -> 119 us  [gradients(): pl.pallas_call(gradients_kernel, out_shape=(jax.ShapeDtypeStruct((2 * ADA...]
    dot_general x8 -> x0, matrix products: 9.8 us -> none  [the longest x2 3.71 us: contract_row_dims(): lax.dot_general(left, right, (((0,), (0,)), ((), ())), preferred_element_...]
    unnamed x24 -> x10, local copies, waits for them, and re-layouts: 3.66 us -> 0.87 us
    another operation x4 -> x2, other arithmetic: 2.86 us -> 0.88 us  [the longest x1 0.8 us: per_device(): ad = jnp.stack([up_adapter_second, down_adapter_first.T])]
where the time goes in v2:
time: 128 us; the launch traced here: 127 us
  Pallas kernels  119 us (93%)
  local copies, waits for them, and re-layouts  5.22 us (4%)
  between operations  1.37 us (1%)
    pallas_call x1, Pallas kernels, gradients(): pl.pallas_call(gradients_kernel, out_shape=(jax.ShapeDtypeStruct((2 * ADA...  119 us

profile of v2, /device:TPU:6, one launch (start us, length us, event | category | flops | bytes accessed | tf_op | source)
XLA Modules:
  0.0 126.9 jit_solution(4079312140812123463)
XLA Ops:
  0.6 0.0 copy-start
  1.3 0.2 copy-done
  1.6 0.1 dynamic-slice_bitcast_fusion.1
  1.7 0.8 dynamic-slice_bitcast_fusion
  2.4 0.0 copy-start.4
  2.4 0.1 pad_maximum_fusion
  2.5 0.6 copy-done.4
  3.1 0.6 reshape.11.gain
  3.8 0.2 copy.17
  3.9 0.0 copy-start.1
  3.9 0.0 copy-start.2
  3.9 0.7 pad.8.adp
  4.7 0.0 copy-done.1
  4.7 0.0 copy-done.2
  4.7 0.8 fusion.5.ad
  5.5 119.4 %gradients.1 = (f32[32,160]{1,0:T(8,128)}, f32[32,27]{1,0:T(8,128)}) custom-call(s32[1]{0:T(128)S(6)} %copy.18.lengths, bf16[256,640]{1,0:T(8,128)(2,1)} %xin.1, bf16[256,640]{1,0:T(8,128)(2,1)} %gin.1, bf16[8,640]{1,0:T(8,128)(2,1)} %reshape.11.gain, bf16[160,864]{1,0:T(8,128)(2,1)} %wg.1, bf16[160,864]{1,0:T(8,128)(2,1)} %wu.1, bf16[160,864]{1,0:T(8,128)(2,1)} %wd.1, ...), custom_call_target="tpu_custom_call" | custom-call | tf_op jit(solution)/shard_map/gradients/pallas_call | solution.py:493
  124.9 0.0 copy-start.3
  124.9 1.4 %fusion.7 = (f32[16,160]{1,0:T(8,128)}, f32[160,16]{0,1:T(8,128)}) fusion(f32[32,160]{1,0:T(8,128)} %get-tuple-element.6), kind=kLoop, calls=%fused_computation.15 | loop fusion | bytes 40960 | tf_op jit(solution)/shard_map/slice | solution.py:587
  126.3 0.0 copy-done.3
  126.3 0.6 slice_bitcast_fusion.1
  (1 shorter events, 0.0 us)
Async XLA Ops:
  0.6 0.9 copy-start
  2.4 0.7 copy-start.4
  3.9 0.8 copy-start.1
  3.9 0.8 copy-start.2
  124.9 1.4 %copy-start.3 = (f32[32,27]{1,0:T(8,128)S(1)}, f32[32,27]{1,0:T(8,128)}, u32[]{:S(2)}) copy-start(f32[32,27]{1,0:T(8,128)} %get-tuple-element.7) | copy-start | bytes 10372

commit v3 on v2

--- a/solution.py
+++ b/solution.py
@@ -28,8 +28,8 @@
 PIECES = ((0, 0, 0, 896), (1, 0, 0, 896), (2, 1, 384, 512), (2, 1, 0, 384))
 RING = (((0, 0), (0, 1), (1, 0), (1, 1), (2, 0), (2, 1), (3, 0)), ((0, 0), (0, 1), (1, 0), (1, 1), (2, 0), (2, 1), (3, 1)))
 ORDER = (
-    *((0, i) for i in range(7)), *((1, i) for i in range(7)),
-    (2, 0), (2, 1), (2, 2), (2, 3), (3, 0), (3, 1), (2, 4), (2, 5), (3, 2), (3, 3), (2, 6), (3, 4), (3, 5), (3, 6),
+    *((0, i) for i in range(7)), *((1, i) for i in range(6)),
+    (2, 0), (2, 1), (1, 6), (2, 2), (2, 3), (2, 4), (2, 5), (3, 0), (3, 1), (2, 6), (3, 2), (3, 3), (3, 4), (3, 5), (3, 6),
 )
 LANE0 = 768
 SPOT = COLS - LANE0
@@ -58,8 +58,8 @@
 
 
 def gradients_kernel(
-    lengths, xin, gin, gain, wg, wu, wd, adp, ad, u_out, s_out,
-    c, at, wb, xt, a_all, b_all, cs2, cs1, near, cr2, cr1, ps, p_all, lat, hid, full, v, v_all, q, q_all, part, msg, msg_all, us, u_row,
+    lengths, x_in, g_in, w0_in, w1_in, w2_in, up_a, down_b, gain, up_b, down_a, up_a_out, up_b_out, down_a_out, down_b_out,
+    xin, gin, win, window, turn, ad, lsem, c, at, wb, xt, a_all, b_all, cs2, cs1, near, cr2, cr1, ps, p_all, lat, hid, full, v, v_all, q, q_all, part, msg, msg_all, us, u_row,
     bs, br, ays, ayr, loc, axs, axr, ads, adr, c2s, c2r, c1s, c1r, pss, psr, vs, vr, qs, qr, ms, mr, us4, ur4,
 ):
     d, m = lax.axis_index("dp"), lax.axis_index("mp")
@@ -85,13 +85,40 @@
     for k in range(1, NMP):
         signal(bar, d, lax.rem(m + k, NMP))
 
-    def assemble(w, ref):
-        wb[w, :, :COLS] = ref[...]
+    lanes = pl.ds(pl.multiple_of(d * (ROWS // 32) // 4 * 128, 128), SEQ)
+    loads = (
+        (w0_in, win.at[0]),
+        (x_in, xin),
+        (w1_in, win.at[1]),
+        (g_in, gin),
+        (w2_in, win.at[2]),
+        (up_a.at[:, lanes], window.at[0]),
+        (down_b.at[:, lanes], window.at[1]),
+    )
+
+    def load(i):
+        return pltpu.make_async_copy(*loads[i], lsem.at[i])
+
+    for i in range(len(loads)):
+        load(i).start()
+
+    def adapter_rows(i):
+        wide = window[i].astype(F32)
+        rows = jnp.zeros((ADAPTER_RANK, ROWS), F32)
+        for k in range(NY):
+            rows = rows + jnp.where(y == k, wide[:, 32 * k : 32 * k + ROWS], 0.0)
+        turn[...] = jnp.zeros_like(turn)
+        turn[SPOT : SPOT + ADAPTER_RANK, :ROWS] = rows
+        return turn[...].T[:ROWS].astype(BF)
+
+    def assemble(w, beside):
+        wb[w, :, :COLS] = win[w]
         tile = wb[w, :, LANE0:]
         lane = lax.broadcasted_iota(jnp.int32, tile.shape, 1)
-        wb[w, :, LANE0:] = jnp.where(lane < SPOT, tile, adp[w])
-
-    assemble(0, wg)
+        wb[w, :, LANE0:] = jnp.where(lane < SPOT, tile, beside)
+
+    load(0).wait()
+    assemble(0, jnp.zeros((ROWS, 128), BF))
     pl.semaphore_wait(bar, 2 + NY - 1 + NMP - 1)
 
     def rows_of(zz, h, n):
@@ -257,7 +284,13 @@
         inverse = lax.rsqrt(jnp.sum(p_all[...], axis=0)[:1] * (1.0 / MODEL_WIDTH) + norm_eps)
         gains = gain[...].astype(F32).T
         lane = lax.broadcasted_iota(jnp.int32, gains.shape, 1)
-        column = jnp.sum(jnp.where(lane == m, gains, 0.0), axis=1, keepdims=True)
+        column = jnp.concatenate(
+            [
+                jnp.sum(jnp.where(lane == m * (FEATS // 128) + i, gains, 0.0), axis=1, keepdims=True)
+                for i in range(FEATS // 128)
+            ],
+            axis=0,
+        )
         normed = (xt[...] * inverse * column).astype(BF)
         for yy in range(NY):
             at[yy, 0] = normed[yy * ROWS : (yy + 1) * ROWS]
@@ -270,17 +303,27 @@
             at[yy, 1] = masked[yy * ROWS : (yy + 1) * ROWS]
 
     def rest():
+        load(1).wait()
         xt[...] = xin[...].astype(F32).T
         ps[...] = jnp.broadcast_to(jnp.sum(xt[...] * xt[...], axis=0, keepdims=True), ps.shape)
         for k in range(1, NMP):
             p_copy(k).start()
-        assemble(1, wu)
+        load(2).wait()
+        load(5).wait()
+        assemble(1, adapter_rows(0))
         normalize()
         tokens_start(0)
+        load(3).wait()
         mask()
         tokens_start(1)
-        assemble(2, wd)
+        load(4).wait()
+        load(6).wait()
+        assemble(2, adapter_rows(1))
         own_rows()
+        part[...] = jnp.zeros_like(part)
+        ad[...] = jnp.zeros_like(ad)
+        ad[0, SPOT : SPOT + ADAPTER_RANK, :COLS] = up_b[...]
+        ad[1, SPOT : SPOT + ADAPTER_RANK, :COLS] = down_a[...]
 
     def tile_of(i):
         return pl.ds(pl.multiple_of(i * 128, 128), 128)
@@ -351,16 +394,17 @@
         11: [lambda: unit_near(0, 1)],
         12: [lambda: tokens_on(1), lambda: unit_pass(0)],
         13: [lambda: unit_own(0)],
-        15: [lambda: tokens_last(1)],
-        16: [lambda: ring_finish(1), lambda: unit_far(1)],
-        17: [lambda: unit_near(1, 0)],
-        18: [lambda: unit_near(1, 1)],
-        19: [lambda: unit_sum(0)],
-        20: [lambda: unit_pass(1)],
-        21: [lambda: unit_own(1), lambda: tokens_done(1)],
-        27: [lambda: ring_finish(2), lambda: unit_far(2), lambda: unit_near(2, 0), lambda: unit_near(2, 1)],
+        14: [lambda: tokens_last(1)],
+        18: [lambda: ring_finish(1), lambda: unit_far(1)],
+        19: [lambda: unit_near(1, 0)],
+        20: [lambda: unit_near(1, 1)],
+        21: [lambda: unit_sum(0)],
+        22: [lambda: unit_pass(1)],
+        23: [lambda: unit_own(1), lambda: tokens_done(1)],
+        25: [lambda: ring_finish(2), lambda: unit_far(2)],
+        26: [lambda: unit_near(2, 0)],
+        27: [lambda: unit_near(2, 1)],
     }
-    part[...] = jnp.zeros_like(part)
     for at_position, (p, i) in enumerate(ORDER):
         ring_issue(p, i)
         for u in plan.get(at_position, ()):
@@ -444,15 +488,17 @@
         u_row[z] = us[...]
 
     for r in range(4):
-        s_out[r * 8 : r * 8 + 8] = summed[:8, r * 32 : r * 32 + SHARE]
+        part_out = (down_a_out, up_b_out)[r // 2]
+        part_out[r % 2 * 8 : r % 2 * 8 + 8] = summed[:8, r * 32 : r * 32 + SHARE]
 
     for j in range(NZ):
         @pl.when(jnp.logical_not(jnp.logical_and(here, z == j)))
         def _():
             remote(us, u_row.at[j], us4.at[0], ur4.at[j], goal, lax.rem(m + 1, NMP)).wait_recv()
 
-        u_out[4 * j : 4 * j + 4, :128] = u_row[j, :4]
-        u_out[4 * j : 4 * j + 4, 128:] = u_row[j, 4:, : ROWS - 128]
+        u_out = (up_a_out, down_b_out)[j // 4]
+        u_out[j % 4 * 4 : j % 4 * 4 + 4, :128] = u_row[j, :4]
+        u_out[j % 4 * 4 : j % 4 * 4 + 4, 128:] = u_row[j, 4:, : ROWS - 128]
 
     def m_sent(k, carry):
         m_copy(k).wait_send()
@@ -487,18 +533,27 @@
         p_copy(k).wait_send()
 
 
-def gradients(lengths, x, g, gain, wg, wu, wd, adp, ad):
+def gradients(lengths, x, g, wg, wu, wd, up_a, down_b, gain, up_b, down_a):
     vmem = pl.BlockSpec(memory_space=pltpu.VMEM)
     dma = pltpu.SemaphoreType.DMA
     return pl.pallas_call(
         gradients_kernel,
         out_shape=(
-            jax.ShapeDtypeStruct((2 * ADAPTER_RANK, ROWS), F32),
-            jax.ShapeDtypeStruct((2 * ADAPTER_RANK, SHARE), F32),
+            jax.ShapeDtypeStruct((ADAPTER_RANK, ROWS), F32),
+            jax.ShapeDtypeStruct((ADAPTER_RANK, SHARE), F32),
+            jax.ShapeDtypeStruct((ADAPTER_RANK, SHARE), F32),
+            jax.ShapeDtypeStruct((ADAPTER_RANK, ROWS), F32),
         ),
-        in_specs=[pl.BlockSpec(memory_space=pltpu.SMEM), *[vmem] * 8],
-        out_specs=(vmem, vmem),
+        in_specs=[pl.BlockSpec(memory_space=pltpu.SMEM), *[pl.BlockSpec(memory_space=pl.ANY)] * 7, *[vmem] * 3],
+        out_specs=(vmem,) * 4,
         scratch_shapes=[
+            pltpu.VMEM((SEQ, FEATS), BF),
+            pltpu.VMEM((SEQ, FEATS), BF),
+            pltpu.VMEM((3, ROWS, COLS), BF),
+            pltpu.VMEM((2, ADAPTER_RANK, SEQ), BF),
+            pltpu.VMEM((128, SEQ), F32),
+            pltpu.VMEM((2, 128, WIDE), BF),
+            dma((7,)),
             pltpu.VMEM((3, SEQ, WIDE), F32),
             pltpu.VMEM((NY, 2, ROWS, SEQ), BF),
             pltpu.VMEM((3, ROWS, WIDE), BF),
@@ -550,7 +605,7 @@
         ],
         compiler_params=pltpu.CompilerParams(collective_id=0, has_side_effects=True),
         name="gradients",
-    )(lengths, x, g, gain, wg, wu, wd, adp, ad)
+    )(lengths, x, g, wg, wu, wd, up_a, down_b, gain, up_b, down_a)
 
 
 def per_device(
@@ -566,25 +621,20 @@
     down_adapter_first,
     down_adapter_second,
 ):
-    d = lax.axis_index("dp")
-    first = lax.dynamic_slice(up_adapter_first, (d * ROWS, 0), (ROWS, ADAPTER_RANK))
-    second = lax.dynamic_slice(down_adapter_second, (0, d * ROWS), (ADAPTER_RANK, ROWS)).T
-    adp = jnp.stack([jnp.zeros_like(first), first, second])
-    adp = jnp.pad(adp, ((0, 0), (0, 0), (SPOT, 128 - SPOT - ADAPTER_RANK)))
-    ad = jnp.stack([up_adapter_second, down_adapter_first.T])
-    ad = jnp.pad(ad, ((0, 0), (SPOT, 128 - SPOT - ADAPTER_RANK), (0, WIDE - COLS)))
-    u, s = gradients(
+    up_a, up_b, down_a, down_b = gradients(
         lengths,
         residual_input,
         cotangent,
-        norm_gain_vector.reshape(NMP, FEATS),
         gate_projection_weight,
         up_projection_weight,
         down_projection_weight,
-        adp,
-        ad,
+        up_adapter_first.T,
+        down_adapter_second,
+        norm_gain_vector.reshape(MODEL_WIDTH // 128, 128),
+        up_adapter_second,
+        down_adapter_first.T,
     )
-    return (u[:ADAPTER_RANK].T, s[ADAPTER_RANK:], s[:ADAPTER_RANK].T, u[ADAPTER_RANK:])
+    return (up_a.T, up_b, down_a.T, down_b)
 
 
 def solution(mesh):

time: 128 us -> 124 us (0.969)
  local copies, waits for them, and re-layouts: 5.22 us -> 3.15 us
    unnamed x10, local copies, waits for them, and re-layouts: 0.87 us -> 3.15 us
    slice x1 -> x0, local copies, waits for them, and re-layouts: 1.35 us -> none  [per_device(): u[ADAPTER_RANK:]]
where the time goes in v3:
time: 124 us; the launch traced here: 123 us
  Pallas kernels  119 us (96%)
  local copies, waits for them, and re-layouts  3.15 us (3%)
  between operations  1.31 us (1%)
    pallas_call x1, Pallas kernels, gradients(): pl.pallas_call(gradients_kernel, out_shape=(jax.ShapeDtypeStruct((ADAPTER...  119 us
    unnamed x10, local copies, waits for them, and re-layouts  3.15 us

profile of v3, /device:TPU:6, one launch (start us, length us, event | category | flops | bytes accessed | tf_op | source)
XLA Modules:
  0.0 123.3 jit_solution(11191769799718777614)
XLA Ops:
  1.3 118.8 %gradients.1 = (f32[16,160]{1,0:T(8,128)}, f32[16,27]{1,0:T(8,128)}, f32[16,27]{1,0:T(8,128)}, f32[16,160]{1,0:T(8,128)}) custom-call(s32[1]{0:T(128)S(6)} %copy.19.lengths, bf16[256,640]{1,0:T(8,128)(2,1)} %x_in.1, bf16[256,640]{1,0:T(8,128)(2,1)} %g_in.1, bf16[160,864]{1,0:T(8,128)(2,1)} %w0_in.1, bf16[160,864]{1,0:T(8,128)(2,1)} %w1_in.1, ...), custom_call_target="tpu_custom_call" | custom-call | tf_op jit(solution)/shard_map/gradients/pallas_call | solution.py:539
  120.1 0.0 copy-start.2
  120.1 0.0 copy-start.1
  120.1 1.3 %copy.20 = f32[160,16]{0,1:T(8,128)} copy(f32[160,16]{0,1:T(8,128)} %bitcast.7) | data formatting | bytes 20480
  121.5 0.0 copy-done.2
  121.5 0.0 copy-start
  121.5 0.6 copy.21
  122.1 0.0 copy-done.1
  122.1 0.6 copy.22
  122.7 0.0 copy-done
  122.7 0.6 copy.23
Async XLA Ops:
  120.1 1.4 %copy-start.2 = (f32[16,27]{1,0:T(8,128)S(1)}, f32[16,27]{1,0:T(8,128)}, u32[]{:S(2)}) copy-start(f32[16,27]{1,0:T(8,128)} %get-tuple-element.17) | copy-start | bytes 5188
  120.1 2.0 %copy-start.1 = (f32[16,27]{1,0:T(8,128)S(1)}, f32[16,27]{1,0:T(8,128)}, u32[]{:S(2)}) copy-start(f32[16,27]{1,0:T(8,128)} %get-tuple-element.10) | copy-start | bytes 5188
  121.5 1.2 copy-start

commit v4 on v3

--- a/solution.py
+++ b/solution.py
@@ -34,6 +34,7 @@
 LANE0 = 768
 SPOT = COLS - LANE0
 FEATS = MODEL_WIDTH // NMP
+FAR_FIRST = (4, 5, 3, 2, 6, 7, 1)
 SHARE = COLS // NDP
 MESH = pl.DeviceIdType.MESH
 BF, F32 = jnp.bfloat16, jnp.float32
@@ -58,7 +59,7 @@
 
 
 def gradients_kernel(
-    lengths, x_in, g_in, w0_in, w1_in, w2_in, up_a, down_b, gain, up_b, down_a, up_a_out, up_b_out, down_a_out, down_b_out,
+    lengths, x_in, g_in, w0_in, w1_in, w2_in, up_a, down_b, gain, up_b, down_a, u_out, s_out,
     xin, gin, win, window, turn, ad, lsem, c, at, wb, xt, a_all, b_all, cs2, cs1, near, cr2, cr1, ps, p_all, lat, hid, full, v, v_all, q, q_all, part, msg, msg_all, us, u_row,
     bs, br, ays, ayr, loc, axs, axr, ads, adr, c2s, c2r, c1s, c1r, pss, psr, vs, vr, qs, qr, ms, mr, us4, ur4,
 ):
@@ -302,24 +303,30 @@
         for yy in range(NY):
             at[yy, 1] = masked[yy * ROWS : (yy + 1) * ROWS]
 
-    def rest():
+    def tokens_first():
         load(1).wait()
         xt[...] = xin[...].astype(F32).T
         ps[...] = jnp.broadcast_to(jnp.sum(xt[...] * xt[...], axis=0, keepdims=True), ps.shape)
-        for k in range(1, NMP):
+        for k in FAR_FIRST:
             p_copy(k).start()
         load(2).wait()
         load(5).wait()
         assemble(1, adapter_rows(0))
         normalize()
         tokens_start(0)
+
+    def tokens_second():
         load(3).wait()
         mask()
         tokens_start(1)
+
+    def weights_rest():
         load(4).wait()
         load(6).wait()
         assemble(2, adapter_rows(1))
         own_rows()
+
+    def adapters_rest():
         part[...] = jnp.zeros_like(part)
         ad[...] = jnp.zeros_like(ad)
         ad[0, SPOT : SPOT + ADAPTER_RANK, :COLS] = up_b[...]
@@ -347,7 +354,7 @@
 
         lax.fori_loop(0, WIDE // 128, chunk, 0)
         v[0] = spots(lat[0]).astype(BF)
-        for k in range(1, NMP):
+        for k in FAR_FIRST:
             v_copy(0, k).start()
 
     def down_side():
@@ -385,8 +392,11 @@
             part[(j0 + j) * NY + yy, 12:16, : ROWS - 128] = rows[4 * j : 4 * j + 4, 128:]
 
     plan = {
-        1: [rest],
+        1: [tokens_first],
+        2: [tokens_second],
         3: [lambda: tokens_x(0)],
+        4: [weights_rest],
+        5: [adapters_rest],
         6: [lambda: tokens_on(0), lambda: tokens_x(1)],
         8: [lambda: tokens_last(0)],
         9: [lambda: ring_finish(0), lambda: tokens_done(0), lambda: unit_far(0)],
@@ -415,19 +425,19 @@
     unit_near(3, 1)
     unit_pass(2)
     unit_own(2)
+    unit_own(3)
+    unit_pass(3)
     unit_sum(1)
     forward_side()
-    unit_pass(3)
-    unit_own(3)
-    down_side()
     unit_sum(2)
     backward_side(3, WIDE // 128)
     unit_sum(3)
     backward_side(0, 3)
     v[1] = spots(lat[1]).astype(BF)
-    for k in range(1, NMP):
+    for k in FAR_FIRST:
         v_copy(1, k).start()
     v_all[1, m] = v[1]
+    down_side()
 
     for i in range(NDP):
         for r in range(4):
@@ -441,7 +451,7 @@
     features = part[:, 8:, :]
     squares = squares + jnp.sum(jnp.sum(features * features, axis=0), keepdims=True)
     q[...] = jnp.broadcast_to(squares, q.shape)
-    for k in range(1, NMP):
+    for k in FAR_FIRST:
         q_copy(k).start()
     q_all[m] = q[...]
     for k in range(1, NMP):
@@ -455,16 +465,13 @@
         dd = lax.rem(d + k, NDP)
         return remote(msg.at[dd], msg_all.at[d], ms.at[k], mr.at[d], dd, m)
 
-    def m_start(k, carry):
-        m_copy(k).start()
-        return carry
-
     def m_arrive(k, carry):
         dd = lax.rem(d + k, NDP)
         remote(msg.at[0], msg_all.at[dd], ms.at[k], mr.at[dd], dd, m).wait_recv()
         return carry
 
-    lax.fori_loop(1, NDP, m_start, 0)
+    for i in range(NDP - 1):
+        m_copy((i + 12) % (NDP - 1) + 1).start()
     msg_all[d] = msg[d]
     lax.fori_loop(1, NDP, m_arrive, 0)
     summed = jnp.sum(msg_all[...].astype(F32), axis=0)
@@ -488,17 +495,15 @@
         u_row[z] = us[...]
 
     for r in range(4):
-        part_out = (down_a_out, up_b_out)[r // 2]
-        part_out[r % 2 * 8 : r % 2 * 8 + 8] = summed[:8, r * 32 : r * 32 + SHARE]
+        s_out[r * 8 : r * 8 + 8] = summed[:8, r * 32 : r * 32 + SHARE]
 
     for j in range(NZ):
         @pl.when(jnp.logical_not(jnp.logical_and(here, z == j)))
         def _():
             remote(us, u_row.at[j], us4.at[0], ur4.at[j], goal, lax.rem(m + 1, NMP)).wait_recv()
 
-        u_out = (up_a_out, down_b_out)[j // 4]
-        u_out[j % 4 * 4 : j % 4 * 4 + 4, :128] = u_row[j, :4]
-        u_out[j % 4 * 4 : j % 4 * 4 + 4, 128:] = u_row[j, 4:, : ROWS - 128]
+        u_out[4 * j : 4 * j + 4, :128] = u_row[j, :4]
+        u_out[4 * j : 4 * j + 4, 128:] = u_row[j, 4:, : ROWS - 128]
 
     def m_sent(k, carry):
         m_copy(k).wait_send()
@@ -539,13 +544,11 @@
     return pl.pallas_call(
         gradients_kernel,
         out_shape=(
-            jax.ShapeDtypeStruct((ADAPTER_RANK, ROWS), F32),
-            jax.ShapeDtypeStruct((ADAPTER_RANK, SHARE), F32),
-            jax.ShapeDtypeStruct((ADAPTER_RANK, SHARE), F32),
-            jax.ShapeDtypeStruct((ADAPTER_RANK, ROWS), F32),
+            jax.ShapeDtypeStruct((2 * ADAPTER_RANK, ROWS), F32),
+            jax.ShapeDtypeStruct((2 * ADAPTER_RANK, SHARE), F32),
         ),
         in_specs=[pl.BlockSpec(memory_space=pltpu.SMEM), *[pl.BlockSpec(memory_space=pl.ANY)] * 7, *[vmem] * 3],
-        out_specs=(vmem,) * 4,
+        out_specs=(vmem, vmem),
         scratch_shapes=[
             pltpu.VMEM((SEQ, FEATS), BF),
             pltpu.VMEM((SEQ, FEATS), BF),
@@ -608,6 +611,22 @@
     )(lengths, x, g, wg, wu, wd, up_a, down_b, gain, up_b, down_a)
 
 
+def hand_over_kernel(u, s, up_a, up_b, down_a, down_b):
+    up_a[...] = u[:ADAPTER_RANK]
+    down_b[...] = u[ADAPTER_RANK:]
+    down_a[...] = s[:ADAPTER_RANK]
+    up_b[...] = s[ADAPTER_RANK:]
+
+
+def hand_over(u, s):
+    vmem = pl.BlockSpec(memory_space=pltpu.VMEM)
+    of_u = jax.ShapeDtypeStruct((ADAPTER_RANK, ROWS), F32)
+    of_s = jax.ShapeDtypeStruct((ADAPTER_RANK, SHARE), F32)
+    return pl.pallas_call(
+        hand_over_kernel, out_shape=(of_u, of_s, of_s, of_u), in_specs=[vmem] * 2, out_specs=(vmem,) * 4, name="hand_over"
+    )(u, s)
+
+
 def per_device(
     residual_input,
     cotangent,
@@ -621,7 +640,7 @@
     down_adapter_first,
     down_adapter_second,
 ):
-    up_a, up_b, down_a, down_b = gradients(
+    u, s = gradients(
         lengths,
         residual_input,
         cotangent,
@@ -634,6 +653,7 @@
         up_adapter_second,
         down_adapter_first.T,
     )
+    up_a, up_b, down_a, down_b = hand_over(u, s)
     return (up_a.T, up_b, down_a.T, down_b)
 
 

time: 124 us -> 122 us (0.984)
  local copies, waits for them, and re-layouts: 3.15 us -> 0 us
    unnamed x10 -> x0, local copies, waits for them, and re-layouts: 3.15 us -> none
    pallas_call x1 -> x2, Pallas kernels: 119 us -> 120 us  [the longest x1 118 us: gradients(): pl.pallas_call(gradients_kernel, out_shape=(jax.ShapeDtypeStruct((2 * ADA...]
where the time goes in v4:
time: 122 us; the launch traced here: 121 us
  Pallas kernels  120 us (98%)
  between operations  1.29 us (1%)
    pallas_call x1, Pallas kernels, gradients(): pl.pallas_call(gradients_kernel, out_shape=(jax.ShapeDtypeStruct((2 * ADA...  118 us

profile of v4, /device:TPU:6, one launch (start us, length us, event | category | flops | bytes accessed | tf_op | source)
XLA Modules:
  0.0 121.1 jit_solution(15002654467219318385)
XLA Ops:
  1.3 118.5 %gradients.1 = (f32[32,160]{1,0:T(8,128)}, f32[32,27]{1,0:T(8,128)}) custom-call(s32[1]{0:T(128)S(6)} %copy.15.lengths, bf16[256,640]{1,0:T(8,128)(2,1)} %x_in.1, bf16[256,640]{1,0:T(8,128)(2,1)} %g_in.1, bf16[160,864]{1,0:T(8,128)(2,1)} %w0_in.1, bf16[160,864]{1,0:T(8,128)(2,1)} %w1_in.1, bf16[160,864]{1,0:T(8,128)(2,1)} %w2_in.1, ...), custom_call_target="tpu_custom_call" | custom-call | tf_op jit(solution)/shard_map/gradients/pallas_call | solution.py:544
  119.7 1.4 %hand_over.1 = (f32[16,160]{1,0:T(8,128)}, f32[16,27]{1,0:T(8,128)}, f32[16,27]{1,0:T(8,128)}, f32[16,160]{1,0:T(8,128)}) custom-call(f32[32,160]{1,0:T(8,128)} %get-tuple-element.10.u, f32[32,27]{1,0:T(8,128)} %get-tuple-element.11.s), custom_call_target="tpu_custom_call" | custom-call | tf_op jit(solution)/shard_map/hand_over/pallas_call | solution.py:625

commit v5 on v4

--- a/solution.py
+++ b/solution.py
@@ -60,8 +60,8 @@
 
 def gradients_kernel(
     lengths, x_in, g_in, w0_in, w1_in, w2_in, up_a, down_b, gain, up_b, down_a, u_out, s_out,
-    xin, gin, win, window, turn, ad, lsem, c, at, wb, xt, a_all, b_all, cs2, cs1, near, cr2, cr1, ps, p_all, lat, hid, full, v, v_all, q, q_all, part, msg, msg_all, us, u_row,
-    bs, br, ays, ayr, loc, axs, axr, ads, adr, c2s, c2r, c1s, c1r, pss, psr, vs, vr, qs, qr, ms, mr, us4, ur4,
+    xin, gin, win, window, turn, ad, lsem, c, at, wb, xt, a_all, b_all, cs2, cs1, near, cr2, cr1, ps, p_all, lat, hid, full, v, v_all, q, q_all, part, msg, msg_all, factor, factor_all, us, u_row,
+    bs, br, ays, ayr, loc, axs, axr, ads, adr, c2s, c2r, c1s, c1r, pss, psr, vs, vr, qs, qr, ms, mr, fs, fr, us4, ur4,
 ):
     d, m = lax.axis_index("dp"), lax.axis_index("mp")
     z, y, x, core = d // NY, lax.rem(d, NY), m // NC, lax.rem(m, NC)
@@ -398,13 +398,13 @@
         4: [weights_rest],
         5: [adapters_rest],
         6: [lambda: tokens_on(0), lambda: tokens_x(1)],
-        8: [lambda: tokens_last(0)],
-        9: [lambda: ring_finish(0), lambda: tokens_done(0), lambda: unit_far(0)],
-        10: [lambda: unit_near(0, 0)],
-        11: [lambda: unit_near(0, 1)],
-        12: [lambda: tokens_on(1), lambda: unit_pass(0)],
-        13: [lambda: unit_own(0)],
-        14: [lambda: tokens_last(1)],
+        9: [lambda: tokens_last(0)],
+        10: [lambda: ring_finish(0), lambda: tokens_done(0), lambda: unit_far(0)],
+        11: [lambda: unit_near(0, 0)],
+        12: [lambda: unit_near(0, 1)],
+        13: [lambda: tokens_on(1), lambda: unit_pass(0)],
+        14: [lambda: unit_own(0)],
+        15: [lambda: tokens_last(1)],
         18: [lambda: ring_finish(1), lambda: unit_far(1)],
         19: [lambda: unit_near(1, 0)],
         20: [lambda: unit_near(1, 1)],
@@ -421,9 +421,9 @@
             u()
     ring_finish(3)
     unit_far(3)
+    unit_pass(2)
     unit_near(3, 0)
     unit_near(3, 1)
-    unit_pass(2)
     unit_own(2)
     unit_own(3)
     unit_pass(3)
@@ -454,27 +454,36 @@
     for k in FAR_FIRST:
         q_copy(k).start()
     q_all[m] = q[...]
+    msg[...] = part[...].astype(BF)
+
+    def m_copy(k):
+        dd = lax.rem(d + k, NDP)
+        return remote(msg.at[dd], msg_all.at[d], ms.at[k], mr.at[d], dd, m)
+
+    def m_arrive(k, carry):
+        dd = lax.rem(d + k, NDP)
+        remote(msg.at[0], msg_all.at[dd], ms.at[k], mr.at[dd], dd, m).wait_recv()
+        remote(factor, factor_all.at[dd], fs.at[k], fr.at[dd], dd, m).wait_recv()
+        return carry
+
+    for i in range(NDP - 1):
+        m_copy((i + 12) % (NDP - 1) + 1).start()
+    msg_all[d] = msg[d]
     for k in range(1, NMP):
         q_copy(k).wait_recv()
     clip_limit = clip_coefficient * math.sqrt(2.0 * ADAPTER_RANK * (MODEL_WIDTH + HIDDEN_SHARD))
     norm = jnp.sqrt(jnp.sum(q_all[...], axis=0))
-    factor = jnp.minimum(1.0, clip_limit / (norm + 1e-06))[:1, :1]
-    msg[...] = (part[...] * factor[None]).astype(BF)
-
-    def m_copy(k):
+    factor[...] = jnp.minimum(1.0, clip_limit / (norm + 1e-06))[:1]
+
+    def f_copy(k):
         dd = lax.rem(d + k, NDP)
-        return remote(msg.at[dd], msg_all.at[d], ms.at[k], mr.at[d], dd, m)
-
-    def m_arrive(k, carry):
-        dd = lax.rem(d + k, NDP)
-        remote(msg.at[0], msg_all.at[dd], ms.at[k], mr.at[dd], dd, m).wait_recv()
-        return carry
+        return remote(factor, factor_all.at[d], fs.at[k], fr.at[d], dd, m)
 
     for i in range(NDP - 1):
-        m_copy((i + 12) % (NDP - 1) + 1).start()
-    msg_all[d] = msg[d]
+        f_copy((i + 12) % (NDP - 1) + 1).start()
+    factor_all[d] = factor[...]
     lax.fori_loop(1, NDP, m_arrive, 0)
-    summed = jnp.sum(msg_all[...].astype(F32), axis=0)
+    summed = jnp.sum(msg_all[...].astype(F32) * factor_all[...], axis=0)
     us[...] = summed[8:]
 
     goal = m * NY + y
@@ -507,6 +516,7 @@
 
     def m_sent(k, carry):
         m_copy(k).wait_send()
+        f_copy(k).wait_send()
         return carry
 
     lax.fori_loop(1, NDP, m_sent, 0)
@@ -580,6 +590,8 @@
             pltpu.VMEM((NDP, 16, 128), F32),
             pltpu.VMEM((NDP, 16, 128), BF),
             pltpu.VMEM((NDP, 16, 128), BF),
+            pltpu.VMEM((1, 128), F32),
+            pltpu.VMEM((NDP, 1, 128), F32),
             pltpu.VMEM((8, 128), F32),
             pltpu.VMEM((NZ, 8, 128), F32),
             dma((4, 2, 7)),
@@ -601,6 +613,8 @@
             dma((2, NMP - 1)),
             dma((NMP - 1,)),
             dma((NMP - 1,)),
+            dma((NDP,)),
+            dma((NDP,)),
             dma((NDP,)),
             dma((NDP,)),
             dma((NMP,)),

time: 122 us -> 121 us (level)
  no operation moved by 1% of the time
where the time goes in v5:
time: 121 us; the launch traced here: 120 us
  Pallas kernels  119 us (98%)
  between operations  1.29 us (1%)
    pallas_call x1, Pallas kernels, gradients(): pl.pallas_call(gradients_kernel, out_shape=(jax.ShapeDtypeStruct((2 * ADA...  118 us

profile of v5, /device:TPU:6, one launch (start us, length us, event | category | flops | bytes accessed | tf_op | source)
XLA Modules:
  0.0 120.3 jit_solution(17155019222483803252)
XLA Ops:
  1.3 117.7 %gradients.1 = (f32[32,160]{1,0:T(8,128)}, f32[32,27]{1,0:T(8,128)}) custom-call(s32[1]{0:T(128)S(6)} %copy.15.lengths, bf16[256,640]{1,0:T(8,128)(2,1)} %x_in.1, bf16[256,640]{1,0:T(8,128)(2,1)} %g_in.1, bf16[160,864]{1,0:T(8,128)(2,1)} %w0_in.1, bf16[160,864]{1,0:T(8,128)(2,1)} %w1_in.1, bf16[160,864]{1,0:T(8,128)(2,1)} %w2_in.1, ...), custom_call_target="tpu_custom_call" | custom-call | tf_op jit(solution)/shard_map/gradients/pallas_call | solution.py:554
  119.0 1.4 %hand_over.1 = (f32[16,160]{1,0:T(8,128)}, f32[16,27]{1,0:T(8,128)}, f32[16,27]{1,0:T(8,128)}, f32[16,160]{1,0:T(8,128)}) custom-call(f32[32,160]{1,0:T(8,128)} %get-tuple-element.10.u, f32[32,27]{1,0:T(8,128)} %get-tuple-element.11.s), custom_call_target="tpu_custom_call" | custom-call | tf_op jit(solution)/shard_map/hand_over/pallas_call | solution.py:639
